TPU v7x, 256 devices: a whole 4x4x8 slice. The times are simulated.
256 devices in a mesh: user: 64 (over z, x, core), pos: 4 (over y).
Axes of the slice: x: 4, y: 4, z: 8, core: 2. Of those that a mesh axis runs over, the one named last changes fastest.
Arguments:
- events: bfloat16 [65536, 256], P('user'), may hold values from -6 to 6
- owners: int32 [65536], P('user'), may hold values from 0 to 127, as said below
- offsets: int32 [65536], P('user'), may hold values from 0 to 2047, as said below
- w_key: bfloat16 [256, 256], replicated, may hold values from -0.375 to 0.375
- w_value: bfloat16 [256, 256], replicated, may hold values from -0.375 to 0.375
- cache_keys: bfloat16 [128, 6144, 256], P('user', 'pos'), may hold values from -7 to 7
- cache_values: bfloat16 [128, 6144, 256], P('user', 'pos'), may hold values from -6 to 6
- hist_len: int32 [128], P('user'), may hold values from 8 to 4096
- active: int32 [128], P('user'), may hold values 0 or 1
- candidates: bfloat16 [128, 1024, 256], P('user', 'pos'), may hold values from -100 to 100
Outputs:
- new_keys: bfloat16 [128, 6144, 256], P('user', 'pos')
- new_values: bfloat16 [128, 6144, 256], P('user', 'pos')
- attended: bfloat16 [128, 1024, 256], P('user', 'pos')
Inputs may be any that keep to these rules, and one draw needn't show every extreme that they name: Among the events of one aligned block of 1024 (one index of user), at most 32 have owners among the users t * 2 to t * 2 + 1, for every t; in every draw some t receives exactly 32 from every block, and all those events belong to one user of that t. offsets[e] is the number of events before e, in the order of the array, that have the same owner as e.
All inputs are finite; a program needn't handle non-finite values. No bound on the sum of `active` on one device may be relied on, other than what follows from the above.
Results may differ from a plain program's by a relative error of at most 0.0067.
Values may be sent and summed in bfloat16 or wider, within the bound.
No kernel may reach another device: no remote copies, remote signals or barrier semaphores. Data moves between devices by JAX's collectives and lax.ppermute only.
A program may use at most 128 MiB of HBM per device.

v0:
```python
import jax
import jax.numpy as jnp
from jax import lax
from jax.sharding import PartitionSpec as P


def in_blocks(value, dim, devices):
    lengths = value.shape
    tiles = value.reshape(*lengths[:dim], devices, lengths[dim] // devices, *lengths[dim + 1 :])
    return jnp.moveaxis(tiles, dim, 0)


def sent_and_summed(value, axis, dim):
    tiles = in_blocks(value, dim, lax.axis_size(axis))
    arrived = lax.all_to_all(tiles, axis, split_axis=0, concat_axis=0, tiled=True)
    return arrived.sum(axis=0)


def side_by_side(arrays, axis, dim, along):
    columns = [a.reshape(*a.shape[:along], -1) for a in arrays]
    both = jnp.concatenate(columns, axis=along)
    filled, at, outs = (sent_and_summed(both, axis, dim), 0, [])
    for a, column in zip(arrays, columns):
        piece = filled[..., at : at + column.shape[along]]
        outs.append(piece.reshape(*piece.shape[:along], *a.shape[along:]))
        at += column.shape[along]
    return tuple(outs)


def on_device(
    events, owners, offsets, w_key, w_value, cache_keys, cache_values, hist_len, active, candidates
):
    groups = lax.axis_size("user")
    blocks = lax.axis_size("pos")
    users_here = cache_keys.shape[0]
    block_rows = cache_keys.shape[1]
    width = cache_keys.shape[2]
    span = block_rows * blocks
    per_event = events.shape[0]
    capacity = 2 * per_event // groups
    slots = groups * capacity
    dest = owners // users_here
    local_user = owners - dest * users_here
    onehot = (dest[:, None] == jnp.arange(groups, dtype=jnp.int32)[None, :]).astype(jnp.int32)
    rank = jnp.sum(jnp.cumsum(onehot, axis=0) * onehot, axis=1) - 1
    slot = dest * capacity + rank
    source = jnp.full((slots,), -1, jnp.int32).at[slot].set(jnp.arange(per_event, dtype=jnp.int32))
    filled = source >= 0
    picked = jnp.maximum(source, 0)
    tags = jnp.where(filled, (local_user * span + offsets)[picked], -1).reshape(groups, capacity)
    both_weights = jnp.concatenate([w_key, w_value], axis=1)
    raw = jnp.where(filled[:, None], events[picked], 0).reshape(groups, capacity, events.shape[1])
    rows = lax.all_to_all(raw, "user", split_axis=0, concat_axis=0, tiled=True)
    marks = lax.all_to_all(tags, "user", split_axis=0, concat_axis=0, tiled=True)
    made = jnp.einsum("gcf,fe->gce", rows, both_weights, preferred_element_type=jnp.float32)
    arrived = made.astype(jnp.bfloat16)
    arrived_tags = marks
    arrived = arrived.reshape(slots, 2 * width)
    marks = arrived_tags.reshape(slots)
    owner_here = marks // span
    offset_here = marks - owner_here * span
    base = lax.axis_index("pos") * block_rows
    pick_user = owner_here[:, None] == jnp.arange(users_here, dtype=jnp.int32)[None, :]
    hist_here = jnp.sum(jnp.where(pick_user, hist_len[None, :], 0), axis=1)
    place = hist_here + offset_here - base
    good = (marks >= 0) & (place >= 0) & (place < block_rows)
    flat = jnp.where(good, owner_here * block_rows + place, users_here * block_rows).astype(
        jnp.int32
    )
    mapping = (
        jnp.full((users_here * block_rows,), -1, jnp.int32)
        .at[flat]
        .set(jnp.arange(slots, dtype=jnp.int32), mode="drop")
    )
    written = mapping >= 0
    taken = arrived[jnp.maximum(mapping, 0)]
    new_keys = jnp.where(written[:, None], taken[:, :width], cache_keys.reshape(-1, width)).reshape(
        cache_keys.shape
    )
    new_values = jnp.where(
        written[:, None], taken[:, width:], cache_values.reshape(-1, width)
    ).reshape(cache_values.shape)
    queries = lax.all_gather(candidates, "pos", axis=1, tiled=True)
    position = base + jnp.arange(block_rows, dtype=jnp.int32)
    valid_all = (position[None, :] < hist_len[:, None]) | written.reshape(users_here, block_rows)
    scale = width ** (-0.5)
    maxima = []
    sums = []
    partial_rows = []
    for user in range(users_here):
        scores = (
            jnp.einsum(
                "cd,pd->cp", queries[user], new_keys[user], preferred_element_type=jnp.float32
            )
            * scale
        )
        valid = valid_all[user][None, :]
        masked = jnp.where(valid, scores, jnp.float32(-1e30))
        block_max = jnp.max(masked, axis=1)
        expo = jnp.where(valid, jnp.exp(masked - block_max[:, None]), jnp.float32(0.0))
        sums.append(jnp.sum(expo, axis=1))
        maxima.append(block_max)
        weights = expo.astype(jnp.bfloat16)
        partial_rows.append(jnp.dot(weights, new_values[user], preferred_element_type=jnp.float32))
    block_max = jnp.stack(maxima)
    block_sum = jnp.stack(sums)
    parts = jnp.stack(partial_rows)
    top = lax.pmax(block_max, "pos")
    factor = jnp.exp(block_max - top)
    acc, total = side_by_side((parts * factor[..., None], block_sum * factor), "pos", 1, 2)
    flag = active.astype(jnp.float32)[:, None, None]
    attended = (acc / total[..., None] * flag).astype(jnp.bfloat16)
    return (new_keys, new_values, attended)


def solution(mesh):
    placed = (
        P("user", None),
        P("user"),
        P("user"),
        P(),
        P(),
        P("user", "pos", None),
        P("user", "pos", None),
        P("user"),
        P("user"),
        P("user", "pos", None),
    )
    return jax.shard_map(
        on_device,
        mesh=mesh,
        in_specs=placed,
        out_specs=(P("user", "pos", None), P("user", "pos", None), P("user", "pos", None)),
        check_vma=False,
    )
```

profile of v0, /device:TPU:32, one launch (start us, length us, event | category | flops | bytes accessed | tf_op | source)
XLA Modules:
  0.0 189.2 jit_solution(4657960480944892318)
XLA Ops:
  7.2 0.0 copy-start
  7.2 0.8 add_select_fusion.1
  8.0 18.0 %reduce-window.6 = s32[64,8,128]{2,1,0:T(8,128)S(1)} reduce-window(s32[64,8,128]{2,1,0:T(8,128)S(1)} %fusion.24, s32[]{:T(128)} %constant.22.clone.1), window={size=1x1x128 pad=0_0x0_0x127_0}, to_apply=%region_0.1 | reduce-window | flops 8323072 | bytes 524292 | tf_op jit(solution)/shard_map/reduce-window
  26.0 0.1 slice.66
  26.1 0.1 copy.39
  26.3 0.1 copy.40
  26.4 0.1 broadcast_add_fusion
  26.5 0.1 fusion.21
  26.6 0.7 multiply_add_fusion
  27.3 4.3 %scatter_custom_fusion = s32[2048]{0:T(1024)S(1)} fusion(s32[1024]{0:T(1024)S(1)} %get-tuple-element.21, s32[1024]{0:T(1024)S(1)} %iota.23, s32[]{:T(128)} %constant.20.clone.1), kind=kCustom, calls=%fused_computation.78 | custom fusion | bytes 8196 | tf_op jit(solution)/shard_map/scatter | solution.py:47
  31.7 8.6 %gather_fusion = s32[2048]{0:T(1024)S(1)} fusion(s32[1024]{0:T(1024)S(1)} %get-tuple-element.20, s32[2048]{0:T(1024)S(1)} %maximum_clamp_fusion.1), kind=kCustom, calls=%fused_computation | custom fusion | bytes 24576 | tf_op jit(solution)/shard_map/gather | solution.py:50
  40.3 0.7 all_to_all.12
  41.0 11.6 %all-to-all-start = ((s32[64,1,32]{2,1,0:T(1,128)}), s32[64,1,32]{2,1,0:T(1,128)S(1)}, u32[]{:S(2)}, u32[]{:S(2)}) async-start(s32[64,1,32]{2,1,0:T(1,128)} %bitcast.3), calls=%async_computation | async-start | bytes 65536 | tf_op jit(solution)/shard_map/all_to_all | solution.py:54
  52.5 0.0 all-gather.2.cloned.1.call-start
  52.6 0.7 all-gather.2.cloned.1.call-update
  53.3 0.0 copy-done
  53.3 0.0 copy-start.5
  53.3 0.0 copy-start.3
  53.3 0.0 copy-start.4
  53.3 7.5 %gather_fusion.1 = bf16[2048,256]{1,0:T(8,128)(2,1)S(1)} fusion(bf16[1024,256]{1,0:T(8,128)(2,1)S(1)} %copy-done, s32[2048]{0:T(1024)S(1)} %maximum_clamp_fusion.1), kind=kCustom, calls=%fused_computation.1 | custom fusion | bytes 2105344 | tf_op jit(solution)/shard_map/gather | solution.py:52
  60.8 0.1 broadcast_in_dim.117
  60.9 1.2 broadcast_select_fusion
  62.1 0.0 all-to-all-done
  62.2 10.5 %all-to-all-start.1 = ((bf16[64,32,256]{2,1,0:T(8,128)(2,1)}), bf16[64,32,256]{2,1,0:T(8,128)(2,1)}, u32[]{:S(2)}, u32[]{:S(2)}) async-start(bf16[64,32,256]{2,1,0:T(8,128)(2,1)} %broadcast_select_fusion), calls=%async_computation.1 | async-start | bytes 2097152 | tf_op jit(solution)/shard_map/all_to_all | solution.py:53
  72.6 0.1 copy.42
  72.7 0.1 copy.44
  72.8 0.1 and.47
  73.0 0.1 copy.46
  73.0 0.1 div.45
  73.1 0.5 broadcast.274
  73.6 0.7 reduce.11
  74.4 0.1 reshape.209
  74.5 0.0 copy-done.5
  74.5 0.1 fusion.25
  74.6 0.1 compare_select_fusion
  74.7 8.2 %scatter_custom_fusion.1 = s32[3072]{0:T(1024)S(1)} fusion(s32[2048]{0:T(1024)S(1)} %bitcast.74, s32[2048]{0:T(1024)S(1)} %iota.24, s32[]{:T(128)} %constant.20.clone.1), kind=kCustom, calls=%fused_computation.71 | custom fusion | bytes 12292 | tf_op jit(solution)/shard_map/scatter | solution.py:73
  82.9 0.1 compare_or_fusion
  83.0 0.1 slice_reduce_fusion.1
  83.1 17.4 %all-to-all-done.1 = bf16[64,32,256]{2,1,0:T(8,128)(2,1)} async-done(((bf16[64,32,256]{2,1,0:T(8,128)(2,1)}), bf16[64,32,256]{2,1,0:T(8,128)(2,1)}, u32[]{:S(2)}, u32[]{:S(2)}) %all-to-all-start.1) | async-done | bytes 1048608 | tf_op jit(solution)/shard_map/all_to_all | solution.py:53
  100.5 0.0 copy-done.3
  100.5 0.0 copy-done.4
  100.5 1.9 %convolution_convert_fusion = bf16[64,32,512]{2,1,0:T(8,128)(2,1)S(1)} fusion(bf16[64,32,256]{2,1,0:T(8,128)(2,1)} %all-to-all-done.1, bf16[256,256]{1,0:T(8,128)(2,1)S(1)} %copy-done.3, bf16[256,256]{1,0:T(8,128)(2,1)S(1)} %copy-done.4), kind=kOutput, calls=%fused_computation.21 | convolution fusion | flops 538443776 | bytes 3407872 | tf_op jit(solution)/shard_map/gcf,fe->gce/dot_general | solution.py:55
  102.4 13.2 %gather_fusion.2 = bf16[3072,512]{1,0:T(8,128)(2,1)} fusion(bf16[2048,512]{1,0:T(8,128)(2,1)S(1)} %bitcast.57, s32[3072]{0:T(1024)S(1)} %maximum_clamp_fusion), kind=kCustom, calls=%fused_computation.2 | custom fusion | bytes 6303744 | tf_op jit(solution)/shard_map/gather | solution.py:76
  115.6 4.5 %slice_select_fusion = (bf16[3072,256]{1,0:T(8,128)(2,1)S(1)}, bf16[3072,256]{1,0:T(8,128)(2,1)}) fusion(bf16[3072,512]{1,0:T(8,128)(2,1)} %gather_fusion.2, bf16[2,1536,256]{2,1,0:T(8,128)(2,1)} %param.16, pred[3072]{0:T(1024)(128)(4,1)S(1)} %broadcast_compare_fusion, bf16[2,1536,256]{2,1,0:T(8,128)(2,1)} %param.15), kind=kLoop, calls=%fused_computation.22 | loop fusion | flops 1572864 | bytes 9440256 | tf_op jit(solution)/shard_map/jit(_where)/select_n | solution.py:80
  120.1 3.2 %fusion.1 = (f32[1024]{0:T(1024)S(1)}, f32[1536,1024]{1,0:T(8,128)S(1)}) fusion(pred[1536]{0:T(1024)(128)(4,1)S(1)} %get-tuple-element.13, bf16[2,1024,256]{2,1,0:T(8,128)(2,1)} %all-gather.2.cloned.1.call-done, bf16[3072,256]{1,0:T(8,128)(2,1)} %get-tuple-element.19), kind=kOutput, calls=%fused_computation.10 | convolution fusion | flops 810023936 | bytes 7607808 | tf_op jit(solution)/shard_map/cd,pd->cp/dot_general | solution.py:92
  123.3 0.0 copy-start.2
  123.3 0.0 copy-start.6
  123.4 2.0 %fusion.6 = f32[1024,256]{1,0:T(8,128)S(1)} fusion(f32[1536,1024]{1,0:T(8,128)S(1)} %get-tuple-element.25, f32[1024]{0:T(1024)S(1)} %get-tuple-element.24, pred[1536]{0:T(1024)(128)(4,1)S(1)} %get-tuple-element.13, bf16[3072,256]{1,0:T(8,128)(2,1)S(1)} %get-tuple-element.18), kind=kOutput, calls=%fused_computation.15 | convolution fusion | flops 813170688 | bytes 8132608 | tf_op jit(solution)/shard_map/dot_general | solution.py:104
  125.3 0.0 copy-done.2
  125.3 0.0 copy-done.6
  125.3 1.0 fusion
  126.4 3.5 %fusion.2 = (f32[1024]{0:T(1024)S(1)}, f32[1024]{0:T(1024)S(1)}) fusion(f32[1536,1024]{1,0:T(8,128)S(1)} %get-tuple-element.27, f32[1024]{0:T(1024)S(1)} %get-tuple-element.26, pred[1536]{0:T(1024)(128)(4,1)S(1)} %get-tuple-element.12, f32[1024]{0:T(1024)S(1)} %get-tuple-element.24, f32[1536,1024]{1,0:T(8,128)S(1)} %get-tuple-element.25, ...), kind=kLoop, calls=%fused_computation.11 | loop fusion | flops 15726592 | bytes 12602368 | tf_op jit(solution)/shard_map/reduce_sum | solution.py:101
  129.9 3.0 %fusion.8 = f32[1024,256]{1,0:T(8,128)} fusion(f32[1536,1024]{1,0:T(8,128)S(1)} %get-tuple-element.27, f32[1024]{0:T(1024)S(1)} %get-tuple-element.26, pred[1536]{0:T(1024)(128)(4,1)S(1)} %get-tuple-element.12, bf16[3072,256]{1,0:T(8,128)(2,1)S(1)} %get-tuple-element.18), kind=kOutput, calls=%fused_computation.16 | convolution fusion | flops 813170688 | bytes 8132608 | tf_op jit(solution)/shard_map/dot_general | solution.py:104
  132.9 10.9 %pmax.7 = f32[2,1024]{1,0:T(2,128)S(1)} all-reduce(f32[2,1024]{1,0:T(2,128)S(1)} %pad_maximum_fusion), channel_id=1, replica_groups=mesh['user'=64,'pos'=4] {'pos'}, use_global_device_ids=true, to_apply=%region_8.9 | all-reduce | flops 2048 | bytes 16384 | tf_op jit(solution)/shard_map/pmax | solution.py:108
  143.7 0.8 copy.48
  144.5 2.4 %copy.47 = f32[1,4,256,256]{2,0,3,1:T(1,128)S(1)} copy(f32[1,4,256,256]{3,2,1,0:T(8,128)} %bitcast.62) | data formatting | bytes 2097152 | tf_op jit(solution)/shard_map/stack | solution.py:107
  147.0 0.0 copy-start.7
  147.0 2.0 %maximum_multiply_fusion = f32[2,4,256,256]{2,0,3,1:T(2,128)S(1)} fusion(f32[1,4,256,256]{2,0,3,1:T(1,128)S(1)} %copy.48, f32[1,4,256,256]{2,0,3,1:T(1,128)S(1)} %copy.47, f32[2,4,256]{2,0,1:T(2,128)S(1)} %bitcast.69), kind=kLoop, calls=%fused_computation.20 | loop fusion | flops 1048576 | bytes 4202496 | tf_op jit(solution)/shard_map/mul | solution.py:110
  149.0 2.3 %maximum_bitcast_fusion = f32[4,2,256,257]{2,1,3,0:T(2,128)} fusion(f32[2,4,256,1]{2,0,3,1:T(2,128)S(1)} %bitcast.68, f32[2,4,256,256]{2,0,3,1:T(2,128)S(1)} %maximum_multiply_fusion), kind=kLoop, calls=%fused_computation.19 | loop fusion | flops 526336 | bytes 4210688 | tf_op jit(solution)/shard_map/transpose | solution.py:10
  151.3 3.6 %all-to-all-start.2 = ((f32[4,2,256,257]{2,1,3,0:T(2,128)}), f32[4,2,256,257]{2,1,3,0:T(2,128)S(1)}, u32[]{:S(2)}, u32[]{:S(2)}) async-start(f32[4,2,256,257]{2,1,3,0:T(2,128)} %maximum_bitcast_fusion), calls=%async_computation.2 | async-start | bytes 4210688 | tf_op jit(solution)/shard_map/all_to_all | solution.py:15
  154.9 25.0 %all-to-all-done.2 = f32[4,2,256,257]{2,1,3,0:T(2,128)S(1)} async-done(((f32[4,2,256,257]{2,1,3,0:T(2,128)}), f32[4,2,256,257]{2,1,3,0:T(2,128)S(1)}, u32[]{:S(2)}, u32[]{:S(2)}) %all-to-all-start.2) | async-done | bytes 2105376 | tf_op jit(solution)/shard_map/all_to_all | solution.py:15
  179.9 1.2 reduce_sum.52
  181.2 0.3 fusion.19
  181.4 0.9 copy.51
  (22 shorter events, 0.2 us)
Async XLA Ops:
  7.2 46.1 %copy-start = (bf16[1024,256]{1,0:T(8,128)(2,1)S(1)}, bf16[1024,256]{1,0:T(8,128)(2,1)}, u32[]{:S(2)}) copy-start(bf16[1024,256]{1,0:T(8,128)(2,1)} %param.10) | copy-start | bytes 1572868
  41.0 21.2 %all-to-all-start = ((s32[64,1,32]{2,1,0:T(1,128)}), s32[64,1,32]{2,1,0:T(1,128)S(1)}, u32[]{:S(2)}, u32[]{:S(2)}) async-start(s32[64,1,32]{2,1,0:T(1,128)} %bitcast.3), calls=%async_computation | async-start | bytes 65536 | tf_op jit(solution)/shard_map/all_to_all | solution.py:54
  52.5 67.5 %all-gather.2.cloned.1.call-start = ((), (), s32[]{:S(2)}) async-start(), calls=%async_computation.3 | async-start | bytes 1310720 | tf_op jit(solution)/shard_map/all_gather | solution.py:83
  53.3 21.2 %copy-start.5 = (s32[2]{0:T(128)S(1)}, s32[2]{0:T(128)}, u32[]{:S(2)}) copy-start(s32[2]{0:T(128)} %param.17) | copy-start | bytes 28
  53.3 47.2 %copy-start.3 = (bf16[256,256]{1,0:T(8,128)(2,1)S(1)}, bf16[256,256]{1,0:T(8,128)(2,1)}, u32[]{:S(2)}) copy-start(bf16[256,256]{1,0:T(8,128)(2,1)} %param.14) | copy-start | bytes 393220
  53.3 47.1 %copy-start.4 = (bf16[256,256]{1,0:T(8,128)(2,1)S(1)}, bf16[256,256]{1,0:T(8,128)(2,1)}, u32[]{:S(2)}) copy-start(bf16[256,256]{1,0:T(8,128)(2,1)} %param.13) | copy-start | bytes 393220
  62.2 38.3 %all-to-all-start.1 = ((bf16[64,32,256]{2,1,0:T(8,128)(2,1)}), bf16[64,32,256]{2,1,0:T(8,128)(2,1)}, u32[]{:S(2)}, u32[]{:S(2)}) async-start(bf16[64,32,256]{2,1,0:T(8,128)(2,1)} %broadcast_select_fusion), calls=%async_computation.1 | async-start | bytes 2097152 | tf_op jit(solution)/shard_map/all_to_all | solution.py:53
  120.1 9.8 %copy-start.1 = (bf16[3072,256]{1,0:T(8,128)(2,1)}, bf16[3072,256]{1,0:T(8,128)(2,1)S(1)}, u32[]{:S(2)}) copy-start(bf16[3072,256]{1,0:T(8,128)(2,1)S(1)} %get-tuple-element.18) | copy-start | bytes 4718596
  123.3 2.0 %copy-start.2 = (bf16[3072,256]{1,0:T(8,128)(2,1)S(1)}, bf16[3072,256]{1,0:T(8,128)(2,1)}, u32[]{:S(2)}) copy-start(bf16[3072,256]{1,0:T(8,128)(2,1)} %get-tuple-element.19) | copy-start | bytes 4718596
  123.3 2.0 %copy-start.6 = (bf16[2,1024,256]{2,1,0:T(8,128)(2,1)S(1)}, bf16[2,1024,256]{2,1,0:T(8,128)(2,1)}, u32[]{:S(2)}) copy-start(bf16[2,1024,256]{2,1,0:T(8,128)(2,1)} %all-gather.2.cloned.1.call-done) | copy-start | bytes 3145732
  147.0 7.9 %copy-start.7 = (s32[2]{0:T(128)S(1)}, s32[2]{0:T(128)}, u32[]{:S(2)}) copy-start(s32[2]{0:T(128)} %param.18) | copy-start | bytes 28
  151.3 28.7 %all-to-all-start.2 = ((f32[4,2,256,257]{2,1,3,0:T(2,128)}), f32[4,2,256,257]{2,1,3,0:T(2,128)S(1)}, u32[]{:S(2)}, u32[]{:S(2)}) async-start(f32[4,2,256,257]{2,1,3,0:T(2,128)} %maximum_bitcast_fusion), calls=%async_computation.2 | async-start | bytes 4210688 | tf_op jit(solution)/shard_map/all_to_all | solution.py:15
Sparse Core Ops, SparseCore 0:
  55.2 27.9 all-gather.1
where the time goes:
time: 190 us; the launch traced here: 189 us
  local copies, waits for them, and re-layouts  48.2 us (25%)
  waiting for transfers between devices  43.1 us (23%)
  other arithmetic  35.7 us (19%)
  starting transfers between devices  25.7 us (14%)
  between operations  14.4 us (8%)
  matrix products  11.1 us (6%)
  blocking collectives  10.9 us (6%)
    all_to_all x1, waiting for transfers between devices, sent_and_summed(): lax.all_to_all(tiles, axis, split_axis=0, concat_axis=0, tiled=True)  25 us
    another operation x3, other arithmetic  18.2 us
    all_to_all x1, waiting for transfers between devices, on_device(): rows = lax.all_to_all(raw, 'user', split_axis=0, concat_axis=0, tiled=True)  17.4 us
    gather x1, local copies, waits for them, and re-layouts, on_device(): taken = arrived[jnp.maximum(mapping, 0)]  13.2 us
    all_to_all x1, starting transfers between devices, on_device(): lax.all_to_all(tags, 'user', split_axis=0, concat_axis=0, tiled=True)  11.6 us
    pmax x1, blocking collectives, on_device(): top = lax.pmax(block_max, 'pos')  10.9 us
    all_to_all x1, starting transfers between devices, on_device(): rows = lax.all_to_all(raw, 'user', split_axis=0, concat_axis=0, tiled=True)  10.5 us
    gather x1, local copies, waits for them, and re-layouts, on_device(): (local_user * span + offsets)[picked]  8.58 us
  transfers between devices with their start and end apart: 4, of which 2 were waited for; matrix products, arithmetic and copies ran while one was open for 20% of the time, Pallas kernels for 0%

commit v1 on v0

v1 whole, which is shorter than its diff:
```python
import jax
import jax.numpy as jnp
from jax import lax
from jax.experimental import pallas as pl
from jax.experimental.pallas import tpu as pltpu
from jax.sharding import PartitionSpec as P

NEG = -1e30
LOG2E = 1.4426950408889634
bf16 = jnp.bfloat16
f32 = jnp.float32
i32 = jnp.int32
NT = (((1,), (1,)), ((), ()))
ROW = 256
META = 128


def iota(shape, dim):
    return lax.broadcasted_iota(i32, shape, dim)


def split3(x):
    hi = x.astype(bf16)
    rest = x - hi.astype(f32)
    mid = rest.astype(bf16)
    low = (rest - mid.astype(f32)).astype(bf16)
    return hi, mid, low


def route_kernel(cap, groups):
    pieces = cap // 8

    def body(owners, offsets, events, out):
        n = owners.shape[1]
        users = 2 * groups
        own = owners[...]
        off = offsets[...]
        who = iota((users, n), 0)
        mine = who == own
        base = jnp.min(jnp.where(mine, off, jnp.int32(1 << 24)), axis=1, keepdims=True)
        count = jnp.sum(jnp.where(mine, 1.0, 0.0), axis=1, keepdims=True).astype(i32)
        odd = own % 2
        before = (who == own - 1) & (odd == 1)
        shift = jnp.where(mine, -base, 0) + jnp.where(before, count, 0)
        key = (own // 2) * cap + off + jnp.sum(shift, axis=0, keepdims=True)
        rows = groups * 8
        at = iota((rows, 1), 0)
        start = (at // 8) * cap + at % 8
        raw = events[...]
        for c in range(pieces):
            pick = jnp.where(start + 8 * c == key, 1.0, 0.0).astype(bf16)
            got = jnp.dot(pick, raw, preferred_element_type=f32)
            out[:, :, c * ROW : (c + 1) * ROW] = got.astype(bf16).reshape(groups, 8, ROW)
        ones = jnp.ones((n, META), bf16)
        first = jnp.where((at // 8) * 2 == own, 1.0, 0.0).astype(bf16)
        second = jnp.where((at // 8) * 2 + 1 == own, 1.0, 0.0).astype(bf16)
        c0 = jnp.dot(first, ones, preferred_element_type=f32)
        c1 = jnp.dot(second, ones, preferred_element_type=f32)
        both = jnp.where(iota((rows, META), 1) < META // 2, c0, c1)
        out[:, :, pieces * ROW :] = both.astype(bf16).reshape(groups, 8, META)

    return body


def old_kernel(span, scale):
    def body(info, q0, q1, q2, q3, keys, values, r0, r1, r2, r3):
        factor = scale * LOG2E
        users = keys.shape[0]
        cands = q0.shape[1]
        width = keys.shape[2]
        for q, r in ((q1, r1), (q3, r3), (q2, r2), (q0, r0)):
            marks = []
            for u in range(users):
                limit = info[u]
                s = lax.dot_general(q[u], keys[u], NT, preferred_element_type=f32)
                ok = iota((1, span), 1) < limit
                s = jnp.where(ok, s, NEG)
                top = jnp.max(s, axis=1, keepdims=True)
                e = jnp.exp2((s - top) * factor)
                some = (limit > 0).astype(f32)
                total = jnp.sum(e, axis=1, keepdims=True) * some
                part = jnp.dot(e.astype(bf16), values[u], preferred_element_type=f32) * some
                r[u * cands : (u + 1) * cands, :] = part.astype(bf16)
                marks += [top, total]
            lane = iota((cands, 128), 1)
            mat = jnp.zeros((cands, 128), f32)
            for i, v in enumerate(marks):
                mat = jnp.where(lane == i, v, mat)
            rows = mat.T[:8, :]
            hi, mid, low = split3(rows)
            pad = jnp.zeros_like(hi)
            r[users * cands :, :] = jnp.concatenate([hi, mid, low, pad], axis=0)

    return body


GUARD = 64


def new_kernel(cap, groups, span, scale):
    pieces = cap // 8
    slots = groups * 8

    def body(
        info, rows, w, q, r0, r1, r2, r3, keys, values, nk, nv, att,
        flat, place_k, place_v, table, table_s, sem,
    ):
        factor = scale * LOG2E
        users = q.shape[0]
        cands = q.shape[1]
        width = q.shape[2]
        meta = rows[:, :, pieces * ROW :].reshape(slots, META)
        src = iota((groups, slots), 0)
        col = iota((groups, slots), 1)
        lead = (col % 8) == 0
        earlier = jnp.where(lead & (col // 8 < src), 1.0, 0.0).astype(bf16)
        same = jnp.where(lead & (col // 8 == src), 1.0, 0.0).astype(bf16)
        begin = jnp.dot(earlier, meta, preferred_element_type=f32)
        here = jnp.dot(same, meta, preferred_element_type=f32)
        lane = iota((groups, META), 1)
        table[...] = jnp.where(lane % 2 == 0, begin, here).astype(i32)
        send = pltpu.make_async_copy(table, table_s, sem)
        send.start()

        kvs = []
        for c in range(pieces):
            x = rows[:, :, c * ROW : (c + 1) * ROW].reshape(slots, ROW)
            y = jnp.dot(x, w[...], preferred_element_type=f32).astype(bf16)
            flat[c * slots : (c + 1) * slots, :] = y.astype(f32)
            kvs.append(y)

        mt = meta.astype(f32).T
        c0 = mt[0:1, :].astype(i32)
        c1 = mt[META // 2 : META // 2 + 1, :].astype(i32)
        at = iota((1, slots), 1) % 8
        send.wait()

        def put(s, carry):
            n0 = table_s[s, 1]
            for u in range(users):
                n = table_s[s, u * (META // 2) + 1]
                d = info[u] + table_s[s, u * (META // 2)]
                a = 0 if u == 0 else n0

                @pl.when((n > 0) & (d < span) & (d + n > 0))
                def _():
                    for c in range(pieces):
                        slot = iota((8, 128), 0) + 8 * c
                        ok = (slot >= a) & (slot < a + n)
                        to = d - a + 8 * c + GUARD
                        from_row = pl.multiple_of(c * slots + s * 8, 8)
                        for j in range(width // 128):
                            for dst, o in ((place_k, 0), (place_v, width)):
                                v = flat[pl.ds(from_row, 8), o + j * 128 : o + (j + 1) * 128]
                                pltpu.store(dst.at[u, j, pl.ds(to, 8), :], v, mask=ok)
            return carry

        lax.fori_loop(0, groups, put, 0)

        for u in range(users):
            first = info[u]
            count = table_s[groups - 1, u * (META // 2)] + table_s[groups - 1, u * (META // 2) + 1]
            last = first + count
            step = 256
            for b in range(span // step):
                hit = (first < (b + 1) * step) & (last > b * step) & (count > 0)
                at_rows = iota((step, 128), 0) + b * step
                for src_ref, old, out in ((place_k, keys, nk), (place_v, values, nv)):

                    @pl.when(hit)
                    def _():
                        ok = (at_rows >= first) & (at_rows < last)
                        for j in range(width // 128):
                            new = src_ref[u, j, GUARD + b * step : GUARD + (b + 1) * step, :]
                            was = old[u, b * step : (b + 1) * step, j * 128 : (j + 1) * 128]
                            out[u, b * step : (b + 1) * step, j * 128 : (j + 1) * 128] = jnp.where(
                                ok, new, was.astype(f32)
                            ).astype(bf16)

                    @pl.when(jnp.logical_not(hit))
                    def _():
                        out[u, b * step : (b + 1) * step, :] = old[u, b * step : (b + 1) * step, :]

        k_all = jnp.concatenate([y[:, :width] for y in kvs], axis=0)
        v_all = jnp.concatenate([y[:, width:] for y in kvs], axis=0)
        parts = (r0, r1, r2, r3)
        marks = []
        for r in parts:
            m = r[users * cands :, :].astype(f32)
            marks.append(m[0:8] + m[8:16] + m[16:24])
        for u in range(users):
            oks = []
            for c in range(pieces):
                slot = at + 8 * c
                oks.append(slot < c0 if u == 0 else (slot >= c0) & (slot < c0 + c1))
            ok = jnp.concatenate([o.astype(i32) for o in oks], axis=1) > 0
            s = lax.dot_general(q[u], k_all, NT, preferred_element_type=f32)
            s = jnp.where(ok, s, NEG)
            top_new = jnp.max(s, axis=1, keepdims=True)
            tops = jnp.concatenate([m[2 * u : 2 * u + 1] for m in marks], axis=0)
            sums = jnp.concatenate([m[2 * u + 1 : 2 * u + 2] for m in marks], axis=0)
            cols = jnp.concatenate([tops, sums, jnp.zeros((120, cands), f32)], axis=0).T
            top_old = jnp.max(tops, axis=0, keepdims=True)
            top_old = jnp.max(cols[:, 0:4], axis=1, keepdims=True)
            top = jnp.maximum(top_new, top_old)
            e = jnp.where(ok, jnp.exp2((s - top) * factor), 0.0)
            total = jnp.sum(e, axis=1, keepdims=True)
            acc = jnp.dot(e.astype(bf16), v_all, preferred_element_type=f32)
            for i, r in enumerate(parts):
                g = jnp.exp2((cols[:, i : i + 1] - top) * factor)
                total = total + cols[:, 4 + i : 5 + i] * g
                acc = acc + r[u * cands : (u + 1) * cands, :].astype(f32) * g
            live = info[users + u].astype(f32)
            att[u] = (acc / total * live).astype(bf16)

    return body


def on_device(
    events, owners, offsets, w_key, w_value, cache_keys, cache_values, hist_len, active, candidates
):
    groups = lax.axis_size("user")
    blocks = lax.axis_size("pos")
    users = cache_keys.shape[0]
    span = cache_keys.shape[1]
    width = cache_keys.shape[2]
    cands = candidates.shape[1]
    per_event = events.shape[0]
    cap = 2 * per_event // groups
    scale = width ** (-0.5)
    here = lax.axis_index("pos")
    VM = pl.BlockSpec(memory_space=pltpu.VMEM)
    SM = pl.BlockSpec(memory_space=pltpu.SMEM)

    def moved(x, by):
        return lax.ppermute(x, "pos", [(i, (i + by) % blocks) for i in range(blocks)])

    q1 = moved(candidates, 1)
    q3 = moved(candidates, 3)
    q2 = moved(candidates, 2)

    wide = cap // 8 * ROW + META
    sent = pl.pallas_call(
        route_kernel(cap, groups),
        out_shape=jax.ShapeDtypeStruct((groups, 8, wide), bf16),
        in_specs=[VM] * 3,
        out_specs=VM,
        name="route",
    )(owners.reshape(1, -1), offsets.reshape(1, -1), events)
    rows = lax.all_to_all(sent, "user", split_axis=0, concat_axis=0, tiled=True)

    info = jnp.concatenate([hist_len - here * span, active]).astype(i32)
    r0, r1, r2, r3 = pl.pallas_call(
        old_kernel(span, scale),
        out_shape=[jax.ShapeDtypeStruct((users * cands + 32, width), bf16)] * 4,
        in_specs=[SM] + [VM] * 6,
        out_specs=[VM] * 4,
        name="old",
    )(info, candidates, q1, q2, q3, cache_keys, cache_values)
    b1 = moved(r1, blocks - 1)
    b3 = moved(r3, blocks - 3)
    b2 = moved(r2, blocks - 2)

    w = jnp.concatenate([w_key, w_value], axis=1)
    nk, nv, att = pl.pallas_call(
        new_kernel(cap, groups, span, scale),
        out_shape=[
            jax.ShapeDtypeStruct(cache_keys.shape, bf16),
            jax.ShapeDtypeStruct(cache_values.shape, bf16),
            jax.ShapeDtypeStruct(candidates.shape, bf16),
        ],
        in_specs=[SM] + [VM] * 9,
        out_specs=[VM] * 3,
        scratch_shapes=[
            pltpu.VMEM((cap * groups, 2 * width), f32),
            pltpu.VMEM((users, width // 128, GUARD + span + 32, 128), f32),
            pltpu.VMEM((users, width // 128, GUARD + span + 32, 128), f32),
            pltpu.VMEM((groups, META), i32),
            pltpu.SMEM((groups, META), i32),
            pltpu.SemaphoreType.DMA,
        ],
        name="new",
    )(info, rows, w, candidates, r0, b1, b2, b3, cache_keys, cache_values)
    return nk, nv, att


def solution(mesh):
    placed = (
        P("user", None),
        P("user"),
        P("user"),
        P(),
        P(),
        P("user", "pos", None),
        P("user", "pos", None),
        P("user"),
        P("user"),
        P("user", "pos", None),
    )
    return jax.shard_map(
        on_device,
        mesh=mesh,
        in_specs=placed,
        out_specs=(P("user", "pos", None), P("user", "pos", None), P("user", "pos", None)),
        check_vma=False,
    )
```

time: 190 us -> 73.2 us (0.39)
  local copies, waits for them, and re-layouts: 48.2 us -> 1.86 us
  other arithmetic: 35.7 us -> 1.31 us
  Pallas kernels: 0 us -> 22.8 us
  waiting for transfers between devices: 43.1 us -> 26.5 us
  between operations: 14.4 us -> 0.84 us
  matrix products: 11.1 us -> 0 us
  blocking collectives: 10.9 us -> 0 us
  starting transfers between devices: 25.7 us -> 18.5 us
    all_to_all x3 -> x1, waiting for transfers between devices: 42.4 us -> 0.01 us  [on_device(): rows = lax.all_to_all(sent, 'user', split_axis=0, concat_axis=0, tiled=True)]
    gather x3 -> x0, local copies, waits for them, and re-layouts: 29.3 us -> none  [the longest x1 13.2 us: on_device(): taken = arrived[jnp.maximum(mapping, 0)]]
    ppermute x0 -> x6, waiting for transfers between devices: none -> 26.5 us  [moved(): lax.ppermute(x, 'pos', [(i, (i + by) % blocks) for i in range(blocks)])]
    pallas_call x0 -> x3, Pallas kernels: none -> 22.8 us  [the longest x1 10.5 us: on_device(): pl.pallas_call(new_kernel(cap, groups, span, scale), out_shape=[jax.Shape...]
    another operation x4 -> x0, other arithmetic: 18.2 us -> none
    all_to_all x3 -> x1, starting transfers between devices: 25.7 us -> 11.7 us  [on_device(): rows = lax.all_to_all(sent, 'user', split_axis=0, concat_axis=0, tiled=True)]
    scatter x2 -> x0, local copies, waits for them, and re-layouts: 12.6 us -> none  [the longest x1 8.24 us: on_device(): mapping = jnp.full((users_here * block_rows,), -1, jnp.int32).at[flat].se...]
    dot_general x5 -> x0, matrix products: 11.1 us -> none  [the longest x2 4.91 us: on_device(): jnp.dot(weights, new_values[user], preferred_element_type=jnp.float32)]
  transfers between devices with their start and end apart: 4 -> 7, of which waited for: 2 -> 5; matrix products, arithmetic and copies ran while one was open for 20% -> 2% of each run, Pallas kernels for 0% -> 11%
where the time goes in v1:
time: 73.2 us; the launch traced here: 71.8 us
  waiting for transfers between devices  26.5 us (36%)
  Pallas kernels  22.8 us (31%)
  starting transfers between devices  18.5 us (25%)
  local copies, waits for them, and re-layouts  1.86 us (3%)
  other arithmetic  1.31 us (2%)
  between operations  0.84 us (1%)
    ppermute x6, waiting for transfers between devices, moved(): lax.ppermute(x, 'pos', [(i, (i + by) % blocks) for i in range(blocks)])  26.5 us
    all_to_all x1, starting transfers between devices, on_device(): rows = lax.all_to_all(sent, 'user', split_axis=0, concat_axis=0, tiled=True)  11.7 us
    pallas_call x1, Pallas kernels, on_device(): pl.pallas_call(new_kernel(cap, groups, span, scale), out_shape=[jax.Shape...  10.5 us
    pallas_call x1, Pallas kernels, on_device(): pl.pallas_call(old_kernel(span, scale), out_shape=[jax.ShapeDtypeStruct((...  8.06 us
    ppermute x6, starting transfers between devices, moved(): lax.ppermute(x, 'pos', [(i, (i + by) % blocks) for i in range(blocks)])  6.74 us
    pallas_call x1, Pallas kernels, on_device(): pl.pallas_call(route_kernel(cap, groups), out_shape=jax.ShapeDtypeStruct(...  4.24 us
    unnamed x24, local copies, waits for them, and re-layouts  1.86 us
  transfers between devices with their start and end apart: 7, of which 5 were waited for; matrix products, arithmetic and copies ran while one was open for 2% of the time, Pallas kernels for 11%

profile of v1, /device:TPU:32, one launch (start us, length us, event | category | flops | bytes accessed | tf_op | source)
XLA Modules:
  0.0 71.8 jit_solution(15982704129160486757)
XLA Ops:
  0.6 4.2 %route.1 = bf16[64,8,1152]{2,1,0:T(8,128)(2,1)} custom-call(s32[1,1024]{1,0:T(1,128)} %bitcast.2, s32[1,1024]{1,0:T(1,128)} %bitcast.3, bf16[1024,256]{1,0:T(8,128)(2,1)} %events.1), custom_call_target="tpu_custom_call" | custom-call | tf_op jit(solution)/shard_map/route/pallas_call | solution.py:243
  4.9 0.0 copy-start.1
  4.9 0.0 copy-start.10
  4.9 0.0 copy-start.11
  4.9 11.7 %all-to-all-start = ((bf16[64,8,1152]{2,1,0:T(8,128)(2,1)}), bf16[64,8,1152]{2,1,0:T(8,128)(2,1)S(1)}, u32[]{:S(2)}, u32[]{:S(2)}) async-start(bf16[64,8,1152]{2,1,0:T(8,128)(2,1)} %route.1), calls=%async_computation | async-start | bytes 2359296 | tf_op jit(solution)/shard_map/all_to_all | solution.py:250
  16.6 0.0 copy-done.1
  16.6 3.1 %collective-permute-start.2 = (bf16[2,256,256]{2,1,0:T(8,128)(2,1)S(1)}, bf16[2,256,256]{2,1,0:T(8,128)(2,1)S(1)}, u32[]{:S(2)}, u32[]{:S(2)}) collective-permute-start(bf16[2,256,256]{2,1,0:T(8,128)(2,1)S(1)} %copy-done.1), channel_id=1, source_target_pairs={{0,3},{1,0},{2,1},{3,2},{4,7},{5,4},{6,5},{7,6},{8,11},{9,8},{10,9... | collective-permute-start | bytes 786440 | tf_op jit(solution)/shard_map/ppermute | solution.py:236
  19.7 0.6 collective-permute-start.1
  20.3 1.0 %collective-permute-start = (bf16[2,256,256]{2,1,0:T(8,128)(2,1)S(1)}, bf16[2,256,256]{2,1,0:T(8,128)(2,1)S(1)}, u32[]{:S(2)}, u32[]{:S(2)}) collective-permute-start(bf16[2,256,256]{2,1,0:T(8,128)(2,1)S(1)} %copy-done.1), channel_id=1, source_target_pairs={{0,1},{1,2},{2,3},{3,0},{4,5},{5,6},{6,7},{7,4},{8,9},{9,10},{10,1... | collective-permute-start | bytes 786440 | tf_op jit(solution)/shard_map/ppermute | solution.py:236
  21.3 0.0 copy-done.10
  21.3 0.0 copy-done.11
  21.3 0.6 pad_add_fusion.info
  21.9 0.0 copy-start.8
  21.9 0.0 copy-start.9
  21.9 9.3 %collective-permute-done.2.q3 = bf16[2,256,256]{2,1,0:T(8,128)(2,1)S(1)} collective-permute-done((bf16[2,256,256]{2,1,0:T(8,128)(2,1)S(1)}, bf16[2,256,256]{2,1,0:T(8,128)(2,1)S(1)}, u32[]{:S(2)}, u32[]{:S(2)}) %collective-permute-start.2) | collective-permute-done | bytes 262176 | tf_op jit(solution)/shard_map/ppermute | solution.py:236
  31.2 0.0 copy-start.5
  31.2 0.0 collective-permute-done.1.q2
  31.2 0.0 copy-start.6
  31.2 3.7 %collective-permute-done.q1 = bf16[2,256,256]{2,1,0:T(8,128)(2,1)S(1)} collective-permute-done((bf16[2,256,256]{2,1,0:T(8,128)(2,1)S(1)}, bf16[2,256,256]{2,1,0:T(8,128)(2,1)S(1)}, u32[]{:S(2)}, u32[]{:S(2)}) %collective-permute-start) | collective-permute-done | bytes 262176 | tf_op jit(solution)/shard_map/ppermute | solution.py:236
  34.9 0.0 copy-done.5
  34.9 0.0 copy-done.6
  34.9 0.0 copy-start.7
  34.9 0.7 copy-done.7
  35.6 8.1 %old.1 = (bf16[544,256]{1,0:T(8,128)(2,1)}, bf16[544,256]{1,0:T(8,128)(2,1)}, bf16[544,256]{1,0:T(8,128)(2,1)}, bf16[544,256]{1,0:T(8,128)(2,1)}) custom-call(s32[4]{0:T(128)} %pad_add_fusion.info, bf16[2,256,256]{2,1,0:T(8,128)(2,1)} %q.1, bf16[2,256,256]{2,1,0:T(8,128)(2,1)} %copy-done.7, bf16[2,256,256]{2,1,0:T(8,128)(2,1)} %copy-done.6, ...), custom_call_target="tpu_custom_call" | custom-call | tf_op jit(solution)/shard_map/old/pallas_call | solution.py:253
  43.7 0.8 %collective-permute-start.3 = (bf16[544,256]{1,0:T(8,128)(2,1)}, bf16[544,256]{1,0:T(8,128)(2,1)S(1)}, u32[]{:S(2)}, u32[]{:S(2)}) collective-permute-start(bf16[544,256]{1,0:T(8,128)(2,1)} %get-tuple-element.8), channel_id=1, source_target_pairs={{0,3},{1,0},{2,1},{3,2},{4,7},{5,4},{6,5},{7,6},{8,11},{9,8},{10,9... | collective-permute-start | bytes 835592 | tf_op jit(solution)/shard_map/ppermute | solution.py:236
  44.4 0.5 collective-permute-start.4
  44.9 0.8 %collective-permute-start.5 = (bf16[544,256]{1,0:T(8,128)(2,1)}, bf16[544,256]{1,0:T(8,128)(2,1)S(1)}, u32[]{:S(2)}, u32[]{:S(2)}) collective-permute-start(bf16[544,256]{1,0:T(8,128)(2,1)} %get-tuple-element.10), channel_id=1, source_target_pairs={{0,1},{1,2},{2,3},{3,0},{4,5},{5,6},{6,7},{7,4},{8,9},{9,10},{10,1... | collective-permute-start | bytes 835592 | tf_op jit(solution)/shard_map/ppermute | solution.py:236
  45.7 0.0 copy-done.8
  45.7 0.0 copy-done.9
  45.7 0.7 %pad_maximum_fusion.w = bf16[256,512]{1,0:T(8,128)(2,1)} fusion(bf16[256,256]{1,0:T(8,128)(2,1)S(1)} %copy-done.8, bf16[256,256]{1,0:T(8,128)(2,1)S(1)} %copy-done.9), kind=kLoop, calls=%fused_computation | loop fusion | flops 524288 | bytes 524288 | tf_op jit(solution)/shard_map/concatenate | solution.py:264
  46.4 6.9 %collective-permute-done.3.r1 = bf16[544,256]{1,0:T(8,128)(2,1)S(1)} collective-permute-done((bf16[544,256]{1,0:T(8,128)(2,1)}, bf16[544,256]{1,0:T(8,128)(2,1)S(1)}, u32[]{:S(2)}, u32[]{:S(2)}) %collective-permute-start.3) | collective-permute-done | bytes 278560 | tf_op jit(solution)/shard_map/ppermute | solution.py:236
  53.4 0.0 copy-start.2
  53.4 2.3 %collective-permute-done.4.r2 = bf16[544,256]{1,0:T(8,128)(2,1)S(1)} collective-permute-done((bf16[544,256]{1,0:T(8,128)(2,1)}, bf16[544,256]{1,0:T(8,128)(2,1)S(1)}, u32[]{:S(2)}, u32[]{:S(2)}) %collective-permute-start.4) | collective-permute-done | bytes 278560 | tf_op jit(solution)/shard_map/ppermute | solution.py:236
  55.7 0.0 copy-start.3
  55.7 4.3 %collective-permute-done.5.r3 = bf16[544,256]{1,0:T(8,128)(2,1)S(1)} collective-permute-done((bf16[544,256]{1,0:T(8,128)(2,1)}, bf16[544,256]{1,0:T(8,128)(2,1)S(1)}, u32[]{:S(2)}, u32[]{:S(2)}) %collective-permute-start.5) | collective-permute-done | bytes 278560 | tf_op jit(solution)/shard_map/ppermute | solution.py:236
  60.0 0.0 copy-start.4
  60.0 0.0 all-to-all-done.rows
  60.0 0.0 copy-start
  60.0 0.0 copy-done.2
  60.0 0.0 copy-done.3
  60.0 0.7 copy-done.4
  60.7 0.4 copy-done
  61.2 10.5 %new.1 = (bf16[2,1536,256]{2,1,0:T(8,128)(2,1)}, bf16[2,1536,256]{2,1,0:T(8,128)(2,1)}, bf16[2,256,256]{2,1,0:T(8,128)(2,1)}) custom-call(s32[4]{0:T(128)} %pad_add_fusion.info, bf16[64,8,1152]{2,1,0:T(8,128)(2,1)} %copy-done, bf16[256,512]{1,0:T(8,128)(2,1)} %pad_maximum_fusion.w, bf16[2,256,256]{2,1,0:T(8,128)(2,1)} %q.1, ...), custom_call_target="tpu_custom_call" | custom-call | tf_op jit(solution)/shard_map/new/pallas_call | solution.py:265
  (1 shorter events, 0.0 us)
Async XLA Ops:
  4.9 11.7 %copy-start.1 = (bf16[2,256,256]{2,1,0:T(8,128)(2,1)S(1)}, bf16[2,256,256]{2,1,0:T(8,128)(2,1)}, u32[]{:S(2)}) copy-start(bf16[2,256,256]{2,1,0:T(8,128)(2,1)} %q.1) | copy-start | bytes 786436
  4.9 16.4 %copy-start.10 = (s32[2]{0:T(128)S(1)}, s32[2]{0:T(128)}, u32[]{:S(2)}) copy-start(s32[2]{0:T(128)} %param.17) | copy-start | bytes 28
  4.9 16.4 %copy-start.11 = (s32[2]{0:T(128)S(1)}, s32[2]{0:T(128)}, u32[]{:S(2)}) copy-start(s32[2]{0:T(128)} %param.18) | copy-start | bytes 28
  4.9 55.1 %all-to-all-start = ((bf16[64,8,1152]{2,1,0:T(8,128)(2,1)}), bf16[64,8,1152]{2,1,0:T(8,128)(2,1)S(1)}, u32[]{:S(2)}, u32[]{:S(2)}) async-start(bf16[64,8,1152]{2,1,0:T(8,128)(2,1)} %route.1), calls=%async_computation | async-start | bytes 2359296 | tf_op jit(solution)/shard_map/all_to_all | solution.py:250
  16.6 14.6 %collective-permute-start.2 = (bf16[2,256,256]{2,1,0:T(8,128)(2,1)S(1)}, bf16[2,256,256]{2,1,0:T(8,128)(2,1)S(1)}, u32[]{:S(2)}, u32[]{:S(2)}) collective-permute-start(bf16[2,256,256]{2,1,0:T(8,128)(2,1)S(1)} %copy-done.1), channel_id=1, source_target_pairs={{0,3},{1,0},{2,1},{3,2},{4,7},{5,4},{6,5},{7,6},{8,11},{9,8},{10,9... | collective-permute-start | bytes 786440 | tf_op jit(solution)/shard_map/ppermute | solution.py:236
  19.7 11.5 %collective-permute-start.1 = (bf16[2,256,256]{2,1,0:T(8,128)(2,1)S(1)}, bf16[2,256,256]{2,1,0:T(8,128)(2,1)S(1)}, u32[]{:S(2)}, u32[]{:S(2)}) collective-permute-start(bf16[2,256,256]{2,1,0:T(8,128)(2,1)S(1)} %copy-done.1), channel_id=1, source_target_pairs={{0,2},{1,3},{2,0},{3,1},{4,6},{5,7},{6,4},{7,5},{8,10},{9,11},{10,... | collective-permute-start | bytes 786440 | tf_op jit(solution)/shard_map/ppermute | solution.py:236
  20.3 14.5 %collective-permute-start = (bf16[2,256,256]{2,1,0:T(8,128)(2,1)S(1)}, bf16[2,256,256]{2,1,0:T(8,128)(2,1)S(1)}, u32[]{:S(2)}, u32[]{:S(2)}) collective-permute-start(bf16[2,256,256]{2,1,0:T(8,128)(2,1)S(1)} %copy-done.1), channel_id=1, source_target_pairs={{0,1},{1,2},{2,3},{3,0},{4,5},{5,6},{6,7},{7,4},{8,9},{9,10},{10,1... | collective-permute-start | bytes 786440 | tf_op jit(solution)/shard_map/ppermute | solution.py:236
  21.9 23.8 %copy-start.8 = (bf16[256,256]{1,0:T(8,128)(2,1)S(1)}, bf16[256,256]{1,0:T(8,128)(2,1)}, u32[]{:S(2)}) copy-start(bf16[256,256]{1,0:T(8,128)(2,1)} %param.14) | copy-start | bytes 393220
  21.9 23.8 %copy-start.9 = (bf16[256,256]{1,0:T(8,128)(2,1)S(1)}, bf16[256,256]{1,0:T(8,128)(2,1)}, u32[]{:S(2)}) copy-start(bf16[256,256]{1,0:T(8,128)(2,1)} %param.13) | copy-start | bytes 393220
  31.2 3.7 %copy-start.5 = (bf16[2,256,256]{2,1,0:T(8,128)(2,1)}, bf16[2,256,256]{2,1,0:T(8,128)(2,1)S(1)}, u32[]{:S(2)}) copy-start(bf16[2,256,256]{2,1,0:T(8,128)(2,1)S(1)} %collective-permute-done.2.q3) | copy-start | bytes 786436
  31.2 3.7 %copy-start.6 = (bf16[2,256,256]{2,1,0:T(8,128)(2,1)}, bf16[2,256,256]{2,1,0:T(8,128)(2,1)S(1)}, u32[]{:S(2)}) copy-start(bf16[2,256,256]{2,1,0:T(8,128)(2,1)S(1)} %collective-permute-done.1.q2) | copy-start | bytes 786436
  34.9 0.7 copy-start.7
  43.7 9.7 %collective-permute-start.3 = (bf16[544,256]{1,0:T(8,128)(2,1)}, bf16[544,256]{1,0:T(8,128)(2,1)S(1)}, u32[]{:S(2)}, u32[]{:S(2)}) collective-permute-start(bf16[544,256]{1,0:T(8,128)(2,1)} %get-tuple-element.8), channel_id=1, source_target_pairs={{0,3},{1,0},{2,1},{3,2},{4,7},{5,4},{6,5},{7,6},{8,11},{9,8},{10,9... | collective-permute-start | bytes 835592 | tf_op jit(solution)/shard_map/ppermute | solution.py:236
  44.4 11.3 %collective-permute-start.4 = (bf16[544,256]{1,0:T(8,128)(2,1)}, bf16[544,256]{1,0:T(8,128)(2,1)S(1)}, u32[]{:S(2)}, u32[]{:S(2)}) collective-permute-start(bf16[544,256]{1,0:T(8,128)(2,1)} %get-tuple-element.9), channel_id=1, source_target_pairs={{0,2},{1,3},{2,0},{3,1},{4,6},{5,7},{6,4},{7,5},{8,10},{9,11},{10,... | collective-permute-start | bytes 835592 | tf_op jit(solution)/shard_map/ppermute | solution.py:236
  44.9 15.1 %collective-permute-start.5 = (bf16[544,256]{1,0:T(8,128)(2,1)}, bf16[544,256]{1,0:T(8,128)(2,1)S(1)}, u32[]{:S(2)}, u32[]{:S(2)}) collective-permute-start(bf16[544,256]{1,0:T(8,128)(2,1)} %get-tuple-element.10), channel_id=1, source_target_pairs={{0,1},{1,2},{2,3},{3,0},{4,5},{5,6},{6,7},{7,4},{8,9},{9,10},{10,1... | collective-permute-start | bytes 835592 | tf_op jit(solution)/shard_map/ppermute | solution.py:236
  53.4 6.6 %copy-start.2 = (bf16[544,256]{1,0:T(8,128)(2,1)}, bf16[544,256]{1,0:T(8,128)(2,1)S(1)}, u32[]{:S(2)}) copy-start(bf16[544,256]{1,0:T(8,128)(2,1)S(1)} %collective-permute-done.3.r1) | copy-start | bytes 835588
  55.7 4.3 %copy-start.3 = (bf16[544,256]{1,0:T(8,128)(2,1)}, bf16[544,256]{1,0:T(8,128)(2,1)S(1)}, u32[]{:S(2)}) copy-start(bf16[544,256]{1,0:T(8,128)(2,1)S(1)} %collective-permute-done.4.r2) | copy-start | bytes 835588
  60.0 0.7 %copy-start.4 = (bf16[544,256]{1,0:T(8,128)(2,1)}, bf16[544,256]{1,0:T(8,128)(2,1)S(1)}, u32[]{:S(2)}) copy-start(bf16[544,256]{1,0:T(8,128)(2,1)S(1)} %collective-permute-done.5.r3) | copy-start | bytes 835588
  60.0 1.1 %copy-start = (bf16[64,8,1152]{2,1,0:T(8,128)(2,1)}, bf16[64,8,1152]{2,1,0:T(8,128)(2,1)S(1)}, u32[]{:S(2)}) copy-start(bf16[64,8,1152]{2,1,0:T(8,128)(2,1)S(1)} %all-to-all-done.rows) | copy-start | bytes 3538948

commit v2 on v1

v2 whole, which is shorter than its diff:
```python
import jax
import jax.numpy as jnp
from jax import lax
from jax.experimental import pallas as pl
from jax.experimental.pallas import tpu as pltpu
from jax.sharding import PartitionSpec as P


NEG = -1e30
LOG2E = 1.4426950408889634
bf16 = jnp.bfloat16
f32 = jnp.float32
i32 = jnp.int32
NT = (((1,), (1,)), ((), ()))
ROW = 256
META = 128
HALF = META // 2
GUARD = 64
STEP = 256


def iota(shape, dim):
    return lax.broadcasted_iota(i32, shape, dim)


def split3(x):
    hi = x.astype(bf16)
    rest = x - hi.astype(f32)
    mid = rest.astype(bf16)
    low = (rest - mid.astype(f32)).astype(bf16)
    return hi, mid, low


def fetch(pairs, sems):
    copies = [pltpu.make_async_copy(a, b, sems.at[i]) for i, (a, b) in enumerate(pairs)]
    for copy in copies:
        copy.start()
    return copies


def route_kernel(cap, groups, parts):
    pieces = cap // 8 // parts

    def body(owners_hbm, offsets_hbm, events_hbm, out, owners, offsets, events, sems):
        loads = fetch(((owners_hbm, owners), (offsets_hbm, offsets), (events_hbm, events)), sems)
        part = lax.axis_index("pos") % parts
        n = owners.shape[1]
        users = 2 * groups
        rows = groups * 8
        at = iota((rows, 1), 0)
        pair = (at // 8) * 2
        ones = jnp.ones((n, META), bf16)
        loads[0].wait()
        own = owners[...]
        first = jnp.where(pair == own, 1.0, 0.0).astype(bf16)
        second = jnp.where(pair + 1 == own, 1.0, 0.0).astype(bf16)
        c0 = jnp.dot(first, ones, preferred_element_type=f32)
        c1 = jnp.dot(second, ones, preferred_element_type=f32)
        both = jnp.where(iota((rows, META), 1) < HALF, c0, c1)
        out[:, :, pieces * ROW :] = both.astype(bf16).reshape(groups, 8, META)
        loads[1].wait()
        off = offsets[...]
        who = iota((users, n), 0)
        mine = who == own
        base = jnp.min(jnp.where(mine, off, jnp.int32(1 << 24)), axis=1, keepdims=True)
        count = jnp.sum(jnp.where(mine, 1.0, 0.0), axis=1, keepdims=True).astype(i32)
        before = (who == own - 1) & (own % 2 == 1)
        shift = jnp.where(mine, -base, 0) + jnp.where(before, count, 0)
        key = (own // 2) * cap + off + jnp.sum(shift, axis=0, keepdims=True)
        key = key - part * (cap // parts)
        start = (at // 8) * cap + at % 8
        loads[2].wait()
        raw = events[...]
        for c in range(pieces):
            pick = jnp.where(start + 8 * c == key, 1.0, 0.0).astype(bf16)
            got = jnp.dot(pick, raw, preferred_element_type=f32)
            out[:, :, c * ROW : (c + 1) * ROW] = got.astype(bf16).reshape(groups, 8, ROW)

    return body


def old_kernel(span, scale, chunks, keep):
    def body(hist, *refs):
        qs = refs[:chunks]
        refs = refs[chunks:]
        if keep:
            wk, wv, keys_hbm, values_hbm = refs[:4]
            outs = refs[4 : 4 + chunks]
            w, nk, nv, keys, values, sems, out_sems = refs[4 + chunks :]
        else:
            keys_hbm, values_hbm = refs[:2]
            outs = refs[2 : 2 + chunks]
            keys, values, sems = refs[2 + chunks :]
        users, cands, width = qs[0].shape
        loads = fetch(
            [p for u in range(users) for p in ((keys_hbm.at[u], keys.at[u]), (values_hbm.at[u], values.at[u]))],
            sems,
        )
        factor = scale * LOG2E
        base = lax.axis_index("pos") * span
        if keep:
            w[:, :width] = wk[...]
            w[:, width:] = wv[...]
        stores = []
        for i, (q, r) in enumerate(zip(qs, outs)):
            marks = []
            for u in range(users):
                if i == 0:
                    loads[2 * u].wait()
                    loads[2 * u + 1].wait()
                    if keep:
                        stores += fetch(
                            ((keys.at[u], nk.at[u]), (values.at[u], nv.at[u])), out_sems.at[u]
                        )
                s = lax.dot_general(q[u], keys[u], NT, preferred_element_type=f32)
                s = jnp.where(iota((1, span), 1) < hist[u] - base, s, NEG)
                top = jnp.max(s, axis=1, keepdims=True)
                e = jnp.exp2((s - top) * factor)
                total = jnp.sum(e, axis=1, keepdims=True)
                part = jnp.dot(e.astype(bf16), values[u], preferred_element_type=f32)
                r[u * cands : (u + 1) * cands, :] = part.astype(bf16)
                marks += [top, total]
            lane = iota((cands, 128), 1)
            mat = jnp.zeros((cands, 128), f32)
            for k, v in enumerate(marks):
                mat = jnp.where(lane == k, v, mat)
            rows = mat.T[:8, :]
            hi, mid, low = split3(rows)
            r[users * cands :, :] = jnp.concatenate([hi, mid, low, jnp.zeros_like(hi)], axis=0)
        for copy in stores:
            copy.wait()

    return body


def tables(meta, groups, slots):
    src = iota((groups, slots), 0)
    col = iota((groups, slots), 1)
    lead = (col % 8) == 0
    earlier = jnp.where(lead & (col // 8 < src), 1.0, 0.0).astype(bf16)
    same = jnp.where(lead & (col // 8 == src), 1.0, 0.0).astype(bf16)
    begin = jnp.dot(earlier, meta, preferred_element_type=f32)
    here = jnp.dot(same, meta, preferred_element_type=f32)
    lane = iota((groups, META), 1)
    return jnp.where(lane % 2 == 0, begin, here).astype(i32)


def project(refs, w, flat, slots):
    ys = []
    for c, (ref, lane) in enumerate(refs):
        x = ref[:, :, lane : lane + ROW].reshape(slots, ROW)
        y = jnp.dot(x, w[...], preferred_element_type=f32).astype(bf16)
        flat[c * slots : (c + 1) * slots, :] = y.astype(f32)
        ys.append(y)
    width = w.shape[1] // 2
    keys = jnp.concatenate([y[:, :width] for y in ys], axis=0)
    values = jnp.concatenate([y[:, width:] for y in ys], axis=0)
    return keys, values


def put_rows(hist, base, table_s, flat, place_k, place_v, base_slot, pieces, slots, groups, span):
    users = place_k.shape[0]
    tiles = place_k.shape[1]
    most = GUARD + span

    def put(s, carry):
        n0 = table_s[s, 1]
        for u in range(users):
            n = table_s[s, u * HALF + 1]
            d = hist[u] - base + table_s[s, u * HALF]
            a = 0 if u == 0 else n0
            for c in range(pieces):
                slot = iota((8, 128), 0) + (8 * c + base_slot)
                ok = (slot >= a) & (slot < a + n)
                to = jnp.clip(d - a + (8 * c + base_slot + GUARD), 0, most)
                from_row = pl.multiple_of(c * slots + s * 8, 8)
                for j in range(tiles):
                    for dst, o in ((place_k, 0), (place_v, tiles * 128)):
                        v = flat[pl.ds(from_row, 8), o + j * 128 : o + (j + 1) * 128]
                        pltpu.store(dst.at[u, j, pl.ds(to, 8), :], v, mask=ok)
        return carry

    lax.fori_loop(0, groups, put, 0, unroll=2)


def slot_ends(meta, pieces):
    mt = meta.astype(f32).T
    c0 = mt[0:1, :].astype(i32)
    c1 = mt[HALF : HALF + 1, :].astype(i32)
    end0 = jnp.concatenate([c0] * pieces, axis=1)
    end1 = jnp.concatenate([c0 + c1] * pieces, axis=1)
    return end0, end1


def new_scores(ends, base_slot, pieces, slots, q, keys):
    users, cands, width = q.shape
    end0, end1 = ends
    at = iota((1, slots), 1) % 8 + base_slot
    slot = jnp.concatenate([at + 8 * c for c in range(pieces)], axis=1)
    s = lax.dot_general(
        q[...].reshape(users * cands, width), keys, NT, preferred_element_type=f32
    )
    return jnp.concatenate(
        [
            jnp.where(slot < end0, s[:cands], NEG),
            jnp.where((slot >= end0) & (slot < end1), s[cands:], NEG),
        ],
        axis=0,
    )


def old_marks(olds, users, cands):
    marks = []
    for r in olds:
        m = r[users * cands :, :].astype(f32)
        marks.append(m[0:8] + m[8:16] + m[16:24])
    count = len(olds)
    stack = jnp.concatenate(
        [m[k : k + 1] for k in range(2 * users) for m in marks]
        + [jnp.zeros((128 - 2 * users * count, cands), f32)],
        axis=0,
    ).T
    per = 2 * count
    tops = jnp.concatenate([stack[:, per * u : per * u + count] for u in range(users)], axis=0)
    sums = jnp.concatenate(
        [stack[:, per * u + count : per * u + per] for u in range(users)], axis=0
    )
    return tops, sums


def bounds(hist, base, table_s, groups, u):
    first = hist[u] - base
    count = table_s[groups - 1, u * HALF] + table_s[groups - 1, u * HALF + 1]
    return first, first + count


def near_kernel(cap, groups, span, scale, parts):
    pieces = cap // 8 // parts
    slots = groups * 8

    def body(
        hist, rows, w, q, r0, r1, r3,
        place_k, place_v, acc_out, marks_out, table, ends_out,
        flat, table_s, sem,
    ):
        factor = scale * LOG2E
        users, cands, _ = q.shape
        here = lax.axis_index("pos")
        base = here * span
        base_slot = (here % parts) * (cap // parts)
        meta = rows[:, :, pieces * ROW :].reshape(slots, META)
        table[...] = tables(meta, groups, slots)
        send = pltpu.make_async_copy(table, table_s, sem)
        send.start()
        new_k, new_v = project([(rows, c * ROW) for c in range(pieces)], w, flat, slots)
        ends = slot_ends(meta, pieces)
        for i, row in enumerate(ends):
            ends_out[8 * i : 8 * i + 8, :] = jnp.broadcast_to(row, (8, pieces * slots))
        s = new_scores(ends, base_slot, pieces, slots, q, new_k)
        olds = (r0, r1, r3)
        tops, sums = old_marks(olds, users, cands)
        top = jnp.maximum(
            jnp.max(s, axis=1, keepdims=True), jnp.max(tops, axis=1, keepdims=True)
        )
        e = jnp.exp2((s - top) * factor)
        total = jnp.sum(e, axis=1, keepdims=True)
        acc = jnp.dot(e.astype(bf16), new_v, preferred_element_type=f32)
        for i, r in enumerate(olds):
            g = jnp.exp2((tops[:, i : i + 1] - top) * factor)
            total = total + sums[:, i : i + 1] * g
            acc = acc + r[: users * cands, :].astype(f32) * g
        acc_out[...] = acc
        marks_out[...] = jnp.where(iota((users * cands, 128), 1) == 0, top, total)

        send.wait()
        put_rows(hist, base, table_s, flat, place_k, place_v, base_slot, pieces, slots, groups, span)

    return body


def far_kernel(cap, groups, span, scale, parts):
    pieces = cap // 8 // parts
    slots = groups * 8

    def body(
        hist, active, table, ends, xa, xb, w, q, r2, acc_in, marks_in, pk, pv, nk_in, nv_in,
        place_k, place_v, nk, nv, att,
        flat, out_k, out_v, out_a, table_s, sem, in_sem, out_sem, att_sem,
    ):
        factor = scale * LOG2E
        users, cands, width = q.shape
        here = lax.axis_index("pos")
        base = here * span
        base_slot = (1 - here % parts) * (cap // parts)
        send = pltpu.make_async_copy(table, table_s, sem)
        send.start()
        new_k, new_v = project([(xa, 0), (xb, 0)], w, flat, slots)
        send.wait()
        ins = {}
        for u in range(users):
            first, last = bounds(hist, base, table_s, groups, u)
            for b in range(span // STEP):
                lo, hi = b * STEP, (b + 1) * STEP
                edge = (first < hi) & (last > lo) & ((first > lo) | (last < hi))
                copies = [
                    pltpu.make_async_copy(
                        src.at[u, pl.ds(lo, STEP), :], buf.at[u, pl.ds(lo, STEP), :], in_sem.at[i, u, b]
                    )
                    for i, (src, buf) in enumerate(((nk, out_k), (nv, out_v)))
                ]
                ins[u, b] = edge, copies

                @pl.when(edge)
                def _():
                    for copy in copies:
                        copy.start()

        put_rows(hist, base, table_s, flat, place_k, place_v, base_slot, pieces, slots, groups, span)
        pending = []
        for u in range(users):
            first, last = bounds(hist, base, table_s, groups, u)
            for b in range(span // STEP):
                lo, hi = b * STEP, (b + 1) * STEP
                hit = (first < hi) & (last > lo) & (last > first)
                edge, olds = ins[u, b]
                at = iota((STEP, 128), 0) + lo
                copies = [
                    pltpu.make_async_copy(
                        buf.at[u, pl.ds(lo, STEP), :], out.at[u, pl.ds(lo, STEP), :], out_sem.at[i, u, b]
                    )
                    for i, (buf, out) in enumerate(((out_k, nk), (out_v, nv)))
                ]
                pending.append((hit, copies))

                @pl.when(edge)
                def _():
                    for copy in olds:
                        copy.wait()
                    ok = (at >= first) & (at < last)
                    for j in range(width // 128):
                        lanes = slice(j * 128, (j + 1) * 128)
                        for buf, new in ((out_k, place_k), (out_v, place_v)):
                            was = buf[u, lo:hi, lanes].astype(f32)
                            now = new[u, j, GUARD + lo : GUARD + hi, :]
                            buf[u, lo:hi, lanes] = jnp.where(ok, now, was).astype(bf16)

                @pl.when(hit & jnp.logical_not(edge))
                def _():
                    for j in range(width // 128):
                        lanes = slice(j * 128, (j + 1) * 128)
                        for buf, new in ((out_k, place_k), (out_v, place_v)):
                            now = new[u, j, GUARD + lo : GUARD + hi, :]
                            buf[u, lo:hi, lanes] = now.astype(bf16)

                @pl.when(hit)
                def _():
                    for copy in copies:
                        copy.start()

        s = new_scores((ends[0:1, :], ends[8:9, :]), base_slot, pieces, slots, q, new_k)
        tops, sums = old_marks((r2,), users, cands)
        top_one = marks_in[:, 0:1]
        top = jnp.maximum(jnp.max(s, axis=1, keepdims=True), jnp.maximum(top_one, tops))
        g = jnp.exp2((top_one - top) * factor)
        e = jnp.exp2((s - top) * factor)
        total = jnp.sum(e, axis=1, keepdims=True) + marks_in[:, 1:2] * g
        acc = jnp.dot(e.astype(bf16), new_v, preferred_element_type=f32) + acc_in[...] * g
        g = jnp.exp2((tops - top) * factor)
        total = total + sums * g
        acc = acc + r2[: users * cands, :].astype(f32) * g
        acc = acc * (1.0 / total)
        finals = []
        for u in range(users):
            live = active[u].astype(f32)
            out_a[u] = (acc[u * cands : (u + 1) * cands] * live).astype(bf16)
            finals.append(pltpu.make_async_copy(out_a.at[u], att.at[u], att_sem.at[u]))
            finals[-1].start()

        for hit, copies in pending:

            @pl.when(hit)
            def _():
                for copy in copies:
                    copy.wait()

        for copy in finals:
            copy.wait()

    return body


def on_device(
    events, owners, offsets, w_key, w_value, cache_keys, cache_values, hist_len, active, candidates
):
    groups = lax.axis_size("user")
    blocks = lax.axis_size("pos")
    users, span, width = cache_keys.shape
    cands = candidates.shape[1]
    per_event = events.shape[0]
    cap = 2 * per_event // groups
    parts = 2
    scale = width ** (-0.5)
    VM = pl.BlockSpec(memory_space=pltpu.VMEM)
    SM = pl.BlockSpec(memory_space=pltpu.SMEM)
    HB = pl.BlockSpec(memory_space=pltpu.HBM)

    def moved(x, by):
        return lax.ppermute(x, "pos", [(i, (i + by) % blocks) for i in range(blocks)])

    def shape(*dims, dtype=bf16):
        return jax.ShapeDtypeStruct(dims, dtype)

    def grant(mib):
        return pltpu.CompilerParams(vmem_limit_bytes=mib << 20)

    q1 = moved(candidates, 1)
    q3 = moved(candidates, 3)
    q2 = moved(candidates, 2)

    slots = groups * 8
    pieces = cap // 8 // parts
    wide = pieces * ROW + META
    sent = pl.pallas_call(
        route_kernel(cap, groups, parts),
        out_shape=shape(groups, 8, wide),
        in_specs=[HB] * 3,
        out_specs=VM,
        scratch_shapes=[
            pltpu.VMEM((1, per_event), i32),
            pltpu.VMEM((1, per_event), i32),
            pltpu.VMEM(events.shape, bf16),
            pltpu.SemaphoreType.DMA((3,)),
        ],
        compiler_params=grant(60),
        name="route",
    )(owners.reshape(1, -1), offsets.reshape(1, -1), events)
    rows = lax.all_to_all(sent, "user", split_axis=0, concat_axis=0, tiled=True)

    cache = [
        pltpu.VMEM(cache_keys.shape, bf16),
        pltpu.VMEM(cache_values.shape, bf16),
        pltpu.SemaphoreType.DMA((2 * users,)),
    ]
    part = shape(users * cands + 32, width)
    r1, r3 = pl.pallas_call(
        old_kernel(span, scale, 2, False),
        out_shape=[part] * 2,
        in_specs=[SM] + [VM] * 2 + [HB] * 2,
        out_specs=[VM] * 2,
        scratch_shapes=cache,
        compiler_params=grant(52),
        name="olda",
    )(hist_len, q1, q3, cache_keys, cache_values)
    b1 = moved(r1, blocks - 1)
    b3 = moved(r3, blocks - 3)
    r2, r0, w, nk, nv = pl.pallas_call(
        old_kernel(span, scale, 2, True),
        out_shape=[part] * 2 + [shape(width, 2 * width)] + [shape(*cache_keys.shape)] * 2,
        in_specs=[SM] + [VM] * 4 + [HB] * 2,
        out_specs=[VM] * 3 + [HB] * 2,
        scratch_shapes=cache + [pltpu.SemaphoreType.DMA((users, 2))],
        compiler_params=grant(58),
        name="oldb",
    )(hist_len, q2, candidates, w_key, w_value, cache_keys, cache_values)
    b2 = moved(r2, blocks - 2)

    xa = moved(rows[:, :, :ROW], blocks - 1)
    xb = moved(rows[:, :, ROW : 2 * ROW], 1)
    place = (users, width // 128, GUARD + span + 32, 128)
    pk, pv, acc, marks, table, ends = pl.pallas_call(
        near_kernel(cap, groups, span, scale, parts),
        out_shape=[
            shape(*place, dtype=f32),
            shape(*place, dtype=f32),
            shape(users * cands, width, dtype=f32),
            shape(users * cands, 128, dtype=f32),
            shape(groups, META, dtype=i32),
            shape(16, pieces * slots, dtype=i32),
        ],
        in_specs=[SM] + [VM] * 6,
        out_specs=[VM] * 6,
        scratch_shapes=[
            pltpu.VMEM((pieces * slots, 2 * width), f32),
            pltpu.SMEM((groups, META), i32),
            pltpu.SemaphoreType.DMA,
        ],
        compiler_params=grant(30),
        name="near",
    )(hist_len, rows, w, candidates, r0, b1, b3)
    _, _, nk, nv, att = pl.pallas_call(
        far_kernel(cap, groups, span, scale, parts),
        out_shape=[
            shape(*place, dtype=f32),
            shape(*place, dtype=f32),
            shape(*cache_keys.shape),
            shape(*cache_values.shape),
            shape(*candidates.shape),
        ],
        in_specs=[SM] * 2 + [VM] * 11 + [HB] * 2,
        out_specs=[VM] * 2 + [HB] * 3,
        scratch_shapes=[
            pltpu.VMEM((pieces * slots, 2 * width), f32),
            pltpu.VMEM(cache_keys.shape, bf16),
            pltpu.VMEM(cache_values.shape, bf16),
            pltpu.VMEM(candidates.shape, bf16),
            pltpu.SMEM((groups, META), i32),
            pltpu.SemaphoreType.DMA,
            pltpu.SemaphoreType.DMA((2, users, span // STEP)),
            pltpu.SemaphoreType.DMA((2, users, span // STEP)),
            pltpu.SemaphoreType.DMA((users,)),
        ],
        input_output_aliases={11: 0, 12: 1, 13: 2, 14: 3},
        compiler_params=grant(30),
        name="far",
    )(hist_len, active, table, ends, xa, xb, w, candidates, b2, acc, marks, pk, pv, nk, nv)
    return nk, nv, att


def solution(mesh):
    placed = (
        P("user", None),
        P("user"),
        P("user"),
        P(),
        P(),
        P("user", "pos", None),
        P("user", "pos", None),
        P("user"),
        P("user"),
        P("user", "pos", None),
    )

    return jax.shard_map(
        on_device,
        mesh=mesh,
        in_specs=placed,
        out_specs=(P("user", "pos", None), P("user", "pos", None), P("user", "pos", None)),
        check_vma=False,
    )
```

time: 73.2 us -> 71 us (0.970)
  waiting for transfers between devices: 26.5 us -> 15.8 us
  Pallas kernels: 22.8 us -> 28.1 us
  starting transfers between devices: 18.5 us -> 22.4 us
  other arithmetic: 1.31 us -> 0 us
  local copies, waits for them, and re-layouts: 1.86 us -> 2.65 us
    ppermute x6 -> x8, waiting for transfers between devices: 26.5 us -> 15.8 us  [moved(): lax.ppermute(x, 'pos', [(i, (i + by) % blocks) for i in range(blocks)])]
    pallas_call x3 -> x5, Pallas kernels: 22.8 us -> 28.1 us  [the longest x1 7.04 us: on_device(): pl.pallas_call(old_kernel(span, scale, 2, True), out_shape=[part] * 2 + [...]
    ppermute x6 -> x8, starting transfers between devices: 6.74 us -> 10.8 us  [moved(): lax.ppermute(x, 'pos', [(i, (i + by) % blocks) for i in range(blocks)])]
    concatenate x2 -> x0, other arithmetic: 1.31 us -> none  [the longest x1 0.73 us: on_device(): w = jnp.concatenate([w_key, w_value], axis=1)]
    unnamed x24 -> x12, local copies, waits for them, and re-layouts: 1.86 us -> 2.62 us
  transfers between devices with their start and end apart: 7 -> 9, of which waited for: 5 -> 4; matrix products, arithmetic and copies ran while one was open for 2% -> 0% of each run, Pallas kernels for 11% -> 26%
where the time goes in v2:
time: 71 us; the launch traced here: 69.9 us
  Pallas kernels  28.1 us (40%)
  starting transfers between devices  22.4 us (32%)
  waiting for transfers between devices  15.8 us (22%)
  local copies, waits for them, and re-layouts  2.65 us (4%)
  between operations  0.9 us (1%)
    ppermute x8, waiting for transfers between devices, moved(): lax.ppermute(x, 'pos', [(i, (i + by) % blocks) for i in range(blocks)])  15.8 us
    all_to_all x1, starting transfers between devices, on_device(): rows = lax.all_to_all(sent, 'user', split_axis=0, concat_axis=0, tiled=True)  11.6 us
    ppermute x8, starting transfers between devices, moved(): lax.ppermute(x, 'pos', [(i, (i + by) % blocks) for i in range(blocks)])  10.8 us
    pallas_call x1, Pallas kernels, on_device(): pl.pallas_call(old_kernel(span, scale, 2, True), out_shape=[part] * 2 + [...  7.04 us
    pallas_call x1, Pallas kernels, on_device(): pl.pallas_call(far_kernel(cap, groups, span, scale, parts), out_shape=[sh...  6.89 us
    pallas_call x1, Pallas kernels, on_device(): pl.pallas_call(old_kernel(span, scale, 2, False), out_shape=[part] * 2, i...  5.61 us
    pallas_call x1, Pallas kernels, on_device(): pl.pallas_call(near_kernel(cap, groups, span, scale, parts), out_shape=[s...  5.21 us
    pallas_call x1, Pallas kernels, on_device(): pl.pallas_call(route_kernel(cap, groups, parts), out_shape=shape(groups,...  3.4 us
  transfers between devices with their start and end apart: 9, of which 4 were waited for; matrix products, arithmetic and copies ran while one was open for 0% of the time, Pallas kernels for 26%

profile of v2, /device:TPU:32, one launch (start us, length us, event | category | flops | bytes accessed | tf_op | source)
XLA Modules:
  0.0 69.9 jit_solution(16292886797768317308)
XLA Ops:
  0.6 0.0 copy-start.2
  0.6 3.4 %route.1 = bf16[64,8,640]{2,1,0:T(8,128)(2,1)} custom-call(s32[1,1024]{1,0:T(1,128)} %bitcast.2, s32[1,1024]{1,0:T(1,128)} %bitcast.3, bf16[1024,256]{1,0:T(8,128)(2,1)} %events_hbm.1), custom_call_target="tpu_custom_call" | custom-call | tf_op jit(solution)/shard_map/route/pallas_call | solution.py:423
  4.0 11.6 %all-to-all-start = ((bf16[64,8,640]{2,1,0:T(8,128)(2,1)}), bf16[64,8,640]{2,1,0:T(8,128)(2,1)S(1)}, u32[]{:S(2)}, u32[]{:S(2)}) async-start(bf16[64,8,640]{2,1,0:T(8,128)(2,1)} %route.1), calls=%async_computation | async-start | bytes 1310720 | tf_op jit(solution)/shard_map/all_to_all | solution.py:437
  15.7 3.1 %collective-permute-start.2 = (bf16[2,256,256]{2,1,0:T(8,128)(2,1)}, bf16[2,256,256]{2,1,0:T(8,128)(2,1)S(1)}, u32[]{:S(2)}, u32[]{:S(2)}) collective-permute-start(bf16[2,256,256]{2,1,0:T(8,128)(2,1)} %q.3), channel_id=1, source_target_pairs={{0,3},{1,0},{2,1},{3,2},{4,7},{5,4},{6,5},{7,6},{8,11},{9,8},{10,9... | collective-permute-start | bytes 786440 | tf_op jit(solution)/shard_map/ppermute | solution.py:408
  18.7 0.0 collective-permute-start.1
  18.8 2.2 %collective-permute-start = (bf16[2,256,256]{2,1,0:T(8,128)(2,1)}, bf16[2,256,256]{2,1,0:T(8,128)(2,1)S(1)}, u32[]{:S(2)}, u32[]{:S(2)}) collective-permute-start(bf16[2,256,256]{2,1,0:T(8,128)(2,1)} %q.3), channel_id=1, source_target_pairs={{0,2},{1,3},{2,0},{3,1},{4,6},{5,7},{6,4},{7,5},{8,10},{9,11},{10,... | collective-permute-start | bytes 786440 | tf_op jit(solution)/shard_map/ppermute | solution.py:408
  21.0 9.6 %collective-permute-done.2.refs_1_ = bf16[2,256,256]{2,1,0:T(8,128)(2,1)S(1)} collective-permute-done((bf16[2,256,256]{2,1,0:T(8,128)(2,1)}, bf16[2,256,256]{2,1,0:T(8,128)(2,1)S(1)}, u32[]{:S(2)}, u32[]{:S(2)}) %collective-permute-start.2) | collective-permute-done | bytes 262176 | tf_op jit(solution)/shard_map/ppermute | solution.py:408
  30.5 3.3 %collective-permute-done.1.refs_0_ = bf16[2,256,256]{2,1,0:T(8,128)(2,1)S(1)} collective-permute-done((bf16[2,256,256]{2,1,0:T(8,128)(2,1)}, bf16[2,256,256]{2,1,0:T(8,128)(2,1)S(1)}, u32[]{:S(2)}, u32[]{:S(2)}) %collective-permute-start.1) | collective-permute-done | bytes 262176 | tf_op jit(solution)/shard_map/ppermute | solution.py:408
  33.8 0.0 copy-done.2
  33.8 5.6 %olda.1 = (bf16[544,256]{1,0:T(8,128)(2,1)S(1)}, bf16[544,256]{1,0:T(8,128)(2,1)S(1)}) custom-call(s32[2]{0:T(128)S(1)} %copy-done.2, bf16[2,256,256]{2,1,0:T(8,128)(2,1)S(1)} %collective-permute-done.1.refs_0_, bf16[2,256,256]{2,1,0:T(8,128)(2,1)S(1)} %collective-permute-done.2.refs_1_, bf16[2,1536,256]{2,1,0:T(8,128)(2,1)} %refs_2_.3, ...), custom_call_target="tpu_custom_call" | custom-call | tf_op jit(solution)/shard_map/olda/pallas_call | solution.py:445
  39.5 0.4 collective-permute-start.3
  39.8 0.0 copy-start.3
  39.8 1.7 %collective-permute-start.4 = (bf16[544,256]{1,0:T(8,128)(2,1)S(1)}, bf16[544,256]{1,0:T(8,128)(2,1)S(1)}, u32[]{:S(2)}, u32[]{:S(2)}) collective-permute-start(bf16[544,256]{1,0:T(8,128)(2,1)S(1)} %get-tuple-element.22), channel_id=1, source_target_pairs={{0,1},{1,2},{2,3},{3,0},{4,5},{5,6},{6,7},{7,4},{8,9},{9,10},{10,1... | collective-permute-start | bytes 835592 | tf_op jit(solution)/shard_map/ppermute | solution.py:408
  41.6 0.0 collective-permute-done.refs_0_
  41.6 0.0 copy-start.5
  41.6 0.7 %copy-done.5 = bf16[2,256,256]{2,1,0:T(8,128)(2,1)} copy-done((bf16[2,256,256]{2,1,0:T(8,128)(2,1)}, bf16[2,256,256]{2,1,0:T(8,128)(2,1)S(1)}, u32[]{:S(2)}) %copy-start.5) | copy-done | bytes 262168
  42.3 7.0 %oldb.1 = (bf16[544,256]{1,0:T(8,128)(2,1)}, bf16[544,256]{1,0:T(8,128)(2,1)}, bf16[256,512]{1,0:T(8,128)(2,1)}, bf16[2,1536,256]{2,1,0:T(8,128)(2,1)}, bf16[2,1536,256]{2,1,0:T(8,128)(2,1)}) custom-call(s32[2]{0:T(128)} %hist.7, bf16[2,256,256]{2,1,0:T(8,128)(2,1)} %copy-done.5, bf16[2,256,256]{2,1,0:T(8,128)(2,1)} %q.3, bf16[256,256]{1,0:T(8,128)(2,1)} %refs_2_.2, ...), custom_call_target="tpu_custom_call" | custom-call | tf_op jit(solution)/shard_map/oldb/pallas_call | solution.py:456
  49.3 0.0 copy-start.4
  49.3 0.1 collective-permute-start.7
  49.4 0.0 all-to-all-done.rows
  49.5 2.4 %collective-permute-start.6 = (bf16[64,8,256]{2,1,0:T(8,128)(2,1)S(1)}, bf16[64,8,256]{2,1,0:T(8,128)(2,1)S(1)}, u32[]{:S(2)}, u32[]{:S(2)}) collective-permute-start(bf16[64,8,256]{2,1,0:T(8,128)(2,1)S(1)} %get-tuple-element.35), channel_id=1, source_target_pairs={{0,1},{1,2},{2,3},{3,0},{4,5},{5,6},{6,7},{7,4},{8,9},{9,10},{10,1... | collective-permute-start | bytes 786440 | tf_op jit(solution)/shard_map/ppermute | solution.py:408
  51.9 0.9 %collective-permute-start.5 = (bf16[64,8,256]{2,1,0:T(8,128)(2,1)S(1)}, bf16[64,8,256]{2,1,0:T(8,128)(2,1)S(1)}, u32[]{:S(2)}, u32[]{:S(2)}) collective-permute-start(bf16[64,8,256]{2,1,0:T(8,128)(2,1)S(1)} %get-tuple-element.36), channel_id=1, source_target_pairs={{0,3},{1,0},{2,1},{3,2},{4,7},{5,4},{6,5},{7,6},{8,11},{9,8},{10,9... | collective-permute-start | bytes 786440 | tf_op jit(solution)/shard_map/ppermute | solution.py:408
  52.8 0.0 collective-permute-done.3.r1
  52.8 0.0 collective-permute-done.4.r3
  52.8 0.0 copy-done.3
  52.8 0.0 copy-start
  52.8 0.9 %copy-done = bf16[256,512]{1,0:T(8,128)(2,1)S(1)} copy-done((bf16[256,512]{1,0:T(8,128)(2,1)S(1)}, bf16[256,512]{1,0:T(8,128)(2,1)}, u32[]{:S(2)}) %copy-start) | copy-done | bytes 262168
  53.8 0.0 copy-start.1
  53.8 1.0 %copy-done.1 = bf16[544,256]{1,0:T(8,128)(2,1)S(1)} copy-done((bf16[544,256]{1,0:T(8,128)(2,1)S(1)}, bf16[544,256]{1,0:T(8,128)(2,1)}, u32[]{:S(2)}) %copy-start.1) | copy-done | bytes 278552
  54.7 5.2 %near.1 = (f32[2,2,1632,128]{3,2,1,0:T(8,128)S(1)}, f32[2,2,1632,128]{3,2,1,0:T(8,128)S(1)}, f32[512,256]{1,0:T(8,128)S(1)}, f32[512,128]{1,0:T(8,128)S(1)}, s32...) custom-call(s32[2]{0:T(128)S(1)} %copy-done.3, bf16[64,8,640]{2,1,0:T(8,128)(2,1)S(1)} %all-to-all-done.rows, ...), custom_call_target="tpu_custom_call" | custom-call | tf_op jit(solution)/shard_map/near/pallas_call | solution.py:470
  59.9 0.0 collective-permute-done.7.r2
  59.9 2.6 %collective-permute-done.6.xb = bf16[64,8,256]{2,1,0:T(8,128)(2,1)S(1)} collective-permute-done((bf16[64,8,256]{2,1,0:T(8,128)(2,1)S(1)}, bf16[64,8,256]{2,1,0:T(8,128)(2,1)S(1)}, u32[]{:S(2)}, u32[]{:S(2)}) %collective-permute-start.6) | collective-permute-done | bytes 262176 | tf_op jit(solution)/shard_map/ppermute | solution.py:408
  62.6 0.3 collective-permute-done.5.xa
  62.9 0.0 copy-done.4
  62.9 6.9 %far.1 = (f32[2,2,1632,128]{3,2,1,0:T(8,128)S(1)}, f32[2,2,1632,128]{3,2,1,0:T(8,128)S(1)}, bf16[2,1536,256]{2,1,0:T(8,128)(2,1)}, bf16[2,1536,256]{2,1,0:T(8,128)(2,1)}, bf16[2,256,256]{2,1,0:T(8,128)(2,1)}) custom-call(s32[2]{0:T(128)S(1)} %copy-done.3, ...), custom_call_target="tpu_custom_call", output_to_operand_aliasing={{0}: (11, {}), {1}: (12, {}), {2}: (13, {}), {3}: (14, {})} | custom-call | tf_op jit(solution)/shard_map/far/pallas_call | solution.py:490
  (1 shorter events, 0.0 us)
Async XLA Ops:
  0.6 33.2 %copy-start.2 = (s32[2]{0:T(128)S(1)}, s32[2]{0:T(128)}, u32[]{:S(2)}) copy-start(s32[2]{0:T(128)} %hist.7) | copy-start | bytes 28
  4.0 45.4 %all-to-all-start = ((bf16[64,8,640]{2,1,0:T(8,128)(2,1)}), bf16[64,8,640]{2,1,0:T(8,128)(2,1)S(1)}, u32[]{:S(2)}, u32[]{:S(2)}) async-start(bf16[64,8,640]{2,1,0:T(8,128)(2,1)} %route.1), calls=%async_computation | async-start | bytes 1310720 | tf_op jit(solution)/shard_map/all_to_all | solution.py:437
  15.7 14.9 %collective-permute-start.2 = (bf16[2,256,256]{2,1,0:T(8,128)(2,1)}, bf16[2,256,256]{2,1,0:T(8,128)(2,1)S(1)}, u32[]{:S(2)}, u32[]{:S(2)}) collective-permute-start(bf16[2,256,256]{2,1,0:T(8,128)(2,1)} %q.3), channel_id=1, source_target_pairs={{0,3},{1,0},{2,1},{3,2},{4,7},{5,4},{6,5},{7,6},{8,11},{9,8},{10,9... | collective-permute-start | bytes 786440 | tf_op jit(solution)/shard_map/ppermute | solution.py:408
  18.7 15.1 %collective-permute-start.1 = (bf16[2,256,256]{2,1,0:T(8,128)(2,1)}, bf16[2,256,256]{2,1,0:T(8,128)(2,1)S(1)}, u32[]{:S(2)}, u32[]{:S(2)}) collective-permute-start(bf16[2,256,256]{2,1,0:T(8,128)(2,1)} %q.3), channel_id=1, source_target_pairs={{0,1},{1,2},{2,3},{3,0},{4,5},{5,6},{6,7},{7,4},{8,9},{9,10},{10,1... | collective-permute-start | bytes 786440 | tf_op jit(solution)/shard_map/ppermute | solution.py:408
  18.8 22.8 %collective-permute-start = (bf16[2,256,256]{2,1,0:T(8,128)(2,1)}, bf16[2,256,256]{2,1,0:T(8,128)(2,1)S(1)}, u32[]{:S(2)}, u32[]{:S(2)}) collective-permute-start(bf16[2,256,256]{2,1,0:T(8,128)(2,1)} %q.3), channel_id=1, source_target_pairs={{0,2},{1,3},{2,0},{3,1},{4,6},{5,7},{6,4},{7,5},{8,10},{9,11},{10,... | collective-permute-start | bytes 786440 | tf_op jit(solution)/shard_map/ppermute | solution.py:408
  39.5 13.3 %collective-permute-start.3 = (bf16[544,256]{1,0:T(8,128)(2,1)S(1)}, bf16[544,256]{1,0:T(8,128)(2,1)S(1)}, u32[]{:S(2)}, u32[]{:S(2)}) collective-permute-start(bf16[544,256]{1,0:T(8,128)(2,1)S(1)} %get-tuple-element.21), channel_id=1, source_target_pairs={{0,3},{1,0},{2,1},{3,2},{4,7},{5,4},{6,5},{7,6},{8,11},{9,8},{10,9... | collective-permute-start | bytes 835592 | tf_op jit(solution)/shard_map/ppermute | solution.py:408
  39.8 13.0 %copy-start.3 = (s32[2]{0:T(128)S(1)}, s32[2]{0:T(128)}, u32[]{:S(2)}) copy-start(s32[2]{0:T(128)} %hist.7) | copy-start | bytes 28
  39.8 13.0 %collective-permute-start.4 = (bf16[544,256]{1,0:T(8,128)(2,1)S(1)}, bf16[544,256]{1,0:T(8,128)(2,1)S(1)}, u32[]{:S(2)}, u32[]{:S(2)}) collective-permute-start(bf16[544,256]{1,0:T(8,128)(2,1)S(1)} %get-tuple-element.22), channel_id=1, source_target_pairs={{0,1},{1,2},{2,3},{3,0},{4,5},{5,6},{6,7},{7,4},{8,9},{9,10},{10,1... | collective-permute-start | bytes 835592 | tf_op jit(solution)/shard_map/ppermute | solution.py:408
  41.6 0.7 %copy-start.5 = (bf16[2,256,256]{2,1,0:T(8,128)(2,1)}, bf16[2,256,256]{2,1,0:T(8,128)(2,1)S(1)}, u32[]{:S(2)}) copy-start(bf16[2,256,256]{2,1,0:T(8,128)(2,1)S(1)} %collective-permute-done.refs_0_) | copy-start | bytes 786436
  49.3 13.6 %copy-start.4 = (s32[2]{0:T(128)S(1)}, s32[2]{0:T(128)}, u32[]{:S(2)}) copy-start(s32[2]{0:T(128)} %active.1) | copy-start | bytes 28
  49.3 10.6 %collective-permute-start.7 = (bf16[544,256]{1,0:T(8,128)(2,1)}, bf16[544,256]{1,0:T(8,128)(2,1)S(1)}, u32[]{:S(2)}, u32[]{:S(2)}) collective-permute-start(bf16[544,256]{1,0:T(8,128)(2,1)} %get-tuple-element.25), channel_id=1, source_target_pairs={{0,2},{1,3},{2,0},{3,1},{4,6},{5,7},{6,4},{7,5},{8,10},{9,11},{10,... | collective-permute-start | bytes 835592 | tf_op jit(solution)/shard_map/ppermute | solution.py:408
  49.5 13.1 %collective-permute-start.6 = (bf16[64,8,256]{2,1,0:T(8,128)(2,1)S(1)}, bf16[64,8,256]{2,1,0:T(8,128)(2,1)S(1)}, u32[]{:S(2)}, u32[]{:S(2)}) collective-permute-start(bf16[64,8,256]{2,1,0:T(8,128)(2,1)S(1)} %get-tuple-element.35), channel_id=1, source_target_pairs={{0,1},{1,2},{2,3},{3,0},{4,5},{5,6},{6,7},{7,4},{8,9},{9,10},{10,1... | collective-permute-start | bytes 786440 | tf_op jit(solution)/shard_map/ppermute | solution.py:408
  51.9 11.0 %collective-permute-start.5 = (bf16[64,8,256]{2,1,0:T(8,128)(2,1)S(1)}, bf16[64,8,256]{2,1,0:T(8,128)(2,1)S(1)}, u32[]{:S(2)}, u32[]{:S(2)}) collective-permute-start(bf16[64,8,256]{2,1,0:T(8,128)(2,1)S(1)} %get-tuple-element.36), channel_id=1, source_target_pairs={{0,3},{1,0},{2,1},{3,2},{4,7},{5,4},{6,5},{7,6},{8,11},{9,8},{10,9... | collective-permute-start | bytes 786440 | tf_op jit(solution)/shard_map/ppermute | solution.py:408
  52.8 1.0 %copy-start = (bf16[256,512]{1,0:T(8,128)(2,1)S(1)}, bf16[256,512]{1,0:T(8,128)(2,1)}, u32[]{:S(2)}) copy-start(bf16[256,512]{1,0:T(8,128)(2,1)} %get-tuple-element.19.w) | copy-start | bytes 786436
  53.8 1.0 %copy-start.1 = (bf16[544,256]{1,0:T(8,128)(2,1)S(1)}, bf16[544,256]{1,0:T(8,128)(2,1)}, u32[]{:S(2)}) copy-start(bf16[544,256]{1,0:T(8,128)(2,1)} %get-tuple-element.20.r0) | copy-start | bytes 835588
